TPU v7x, 32 devices: a 4x4x1 block of a 4x4x8 slice. The times are simulated.
32 devices in a mesh: dp: 1 (over z), ep: 32 (over y, x, core).
Axes of the slice: x: 4, y: 4, z: 1, core: 2. Of those that a mesh axis runs over, the one named last changes fastest.
The devices are a block of a 4x4x8 slice.
Arguments:
- x_in: bfloat16 [16384, 256], P(('dp', 'ep'))
- idx_a: int32 [16384, 8], P(('dp', 'ep'))
- idx_b: int32 [16384, 8], P(('dp', 'ep'))
- gate_a: float32 [16384, 8], P(('dp', 'ep'))
- gate_b: float32 [16384, 8], P(('dp', 'ep'))
- dy_out: bfloat16 [16384, 256], P(('dp', 'ep'))
- w1_a: bfloat16 [32, 256, 128], P('ep')
- w3_a: bfloat16 [32, 256, 128], P('ep')
- w2_a: bfloat16 [32, 128, 256], P('ep')
- w1_b: bfloat16 [32, 256, 128], P('ep')
- w3_b: bfloat16 [32, 256, 128], P('ep')
- w2_b: bfloat16 [32, 128, 256], P('ep')
Outputs:
- output 1: bfloat16 [16384, 256], P(('dp', 'ep'))
- output 2: bfloat16 [16384, 256], P(('dp', 'ep'))
- output 3: float32 [32, 256, 128], P(('dp', 'ep'))
- output 4: float32 [32, 256, 128], P(('dp', 'ep'))
- output 5: float32 [32, 128, 256], P(('dp', 'ep'))
- output 6: float32 [32, 256, 128], P(('dp', 'ep'))
- output 7: float32 [32, 256, 128], P(('dp', 'ep'))
- output 8: float32 [32, 128, 256], P(('dp', 'ep'))
- output 9: float32 [16384, 8], P(('dp', 'ep'))
- output 10: float32 [16384, 8], P(('dp', 'ep'))
All inputs are finite; a program needn't handle non-finite values.
Results may differ from a plain program's by a relative error of at most 0.005832.
Values are sent between devices in bfloat16 or wider.
A program may use at most 768 MiB of HBM per device.

v0:
```python
import jax
import jax.numpy as jnp
from jax import lax
from jax.sharding import PartitionSpec as P

CAP_FACTOR = 4


def slot_maps(dev_ids, experts, capacity):
    pair_total = dev_ids.shape[0] * dev_ids.shape[1]
    flat_ids = dev_ids.reshape(-1)
    onehot = (flat_ids[:, None] == jnp.arange(experts, dtype=jnp.int32)[None, :]).astype(jnp.int32)
    pair_slot = jnp.sum(jnp.cumsum(onehot, axis=0) * onehot, axis=1) - 1
    pair_row = flat_ids * capacity + pair_slot
    pair_ids = jnp.arange(pair_total, dtype=jnp.int32)
    row_pair = jnp.full((experts * capacity,), pair_total, jnp.int32).at[pair_row].set(pair_ids)
    return pair_row, row_pair


def send_rows(rows, index, capacity):
    send_buf = jnp.take(rows, index, axis=0, mode="fill", fill_value=0)
    send_buf = send_buf.reshape((index.shape[0] // capacity, capacity) + send_buf.shape[1:])
    return lax.all_to_all(send_buf, "ep", 0, 1, tiled=True)


def send_back(rows):
    back_rows = lax.all_to_all(rows, "ep", 1, 0, tiled=True)
    return back_rows.reshape((back_rows.shape[0] * back_rows.shape[1],) + back_rows.shape[2:])


def expert_forward(u_rows, w_gate, w_up, w_down):
    pre_gate = jnp.einsum("erd,edf->erf", u_rows, w_gate, preferred_element_type=jnp.float32)
    pre_up = jnp.einsum("erd,edf->erf", u_rows, w_up, preferred_element_type=jnp.float32)
    hidden = (jax.nn.silu(pre_gate) * pre_up).astype(jnp.bfloat16)
    out_rows = jnp.einsum("erf,efd->erd", hidden, w_down, preferred_element_type=jnp.float32).astype(jnp.bfloat16)
    return pre_gate, pre_up, hidden, out_rows


def expert_backward(u_rows, dy_rows, gate_rows, w_gate, w_up, w_down):
    pre_gate, pre_up, hidden, out_rows = expert_forward(u_rows, w_gate, w_up, w_down)
    dgate_rows = jnp.einsum("erd,erd->er", dy_rows, out_rows, preferred_element_type=jnp.float32)
    d_out = (gate_rows[:, :, None] * dy_rows).astype(jnp.bfloat16)
    dw_down = jnp.einsum("erf,erd->efd", hidden, d_out, preferred_element_type=jnp.float32)
    d_hidden = jnp.einsum("erd,efd->erf", d_out, w_down, preferred_element_type=jnp.float32)
    gate_sig = jax.nn.sigmoid(pre_gate)
    d_pre_gate = (d_hidden * pre_up * gate_sig * (1.0 + pre_gate * (1.0 - gate_sig))).astype(jnp.bfloat16)
    d_pre_up = (d_hidden * jax.nn.silu(pre_gate)).astype(jnp.bfloat16)
    dw_gate = jnp.einsum("erd,erf->edf", u_rows, d_pre_gate, preferred_element_type=jnp.float32)
    dw_up = jnp.einsum("erd,erf->edf", u_rows, d_pre_up, preferred_element_type=jnp.float32)
    du_rows = (jnp.einsum("erf,edf->erd", d_pre_gate, w_gate, preferred_element_type=jnp.float32) + jnp.einsum("erf,edf->erd", d_pre_up, w_up, preferred_element_type=jnp.float32)).astype(jnp.bfloat16)
    return du_rows, dgate_rows, dw_gate, dw_up, dw_down


def combine(x_rows, gates, back_rows, pair_row):
    tok_dev, top_k = gates.shape
    out_pairs = jnp.take(back_rows, pair_row, axis=0).reshape(tok_dev, top_k, -1)
    branch = jnp.sum(gates[:, :, None] * out_pairs, axis=1)
    return (x_rows.astype(jnp.float32) + branch).astype(jnp.bfloat16)


def layer_backward(dy_rows, u_rows, gates, row_maps, capacity, w_gate, w_up, w_down):
    pair_row, row_pair = row_maps
    tok_dev, top_k = gates.shape
    dy_sent = send_rows(dy_rows, row_pair // top_k, capacity)
    gate_sent = send_rows(gates.reshape(-1), row_pair, capacity)
    u_rows, dy_sent = lax.optimization_barrier((u_rows, dy_sent))
    du_rows, dgate_rows, dw_gate, dw_up, dw_down = expert_backward(u_rows, dy_sent, gate_sent, w_gate, w_up, w_down)
    du_pairs = jnp.take(send_back(du_rows), pair_row, axis=0).reshape(tok_dev, top_k, -1)
    dx_rows = (dy_rows.astype(jnp.float32) + jnp.sum(du_pairs, axis=1, dtype=jnp.float32)).astype(jnp.bfloat16)
    dgate_out = jnp.take(send_back(dgate_rows), pair_row, axis=0).reshape(tok_dev, top_k)
    return dx_rows, dgate_out, (dw_gate, dw_up, dw_down)


def solution(mesh):
    n_group = mesh.shape["ep"]
    tok_spec = P(("dp", "ep"))
    w_spec = P("ep")

    def device_program(x_in, idx_a, idx_b, gate_a, gate_b, dy_out, w1_a, w3_a, w2_a, w1_b, w3_b, w2_b):
        tok_dev, top_k = idx_a.shape
        experts = w1_a.shape[0] * n_group
        capacity = CAP_FACTOR * tok_dev * top_k // experts
        maps_a = slot_maps(idx_a, experts, capacity)
        maps_b = slot_maps(idx_b, experts, capacity)
        u_rows_a = send_rows(x_in, maps_a[1] // top_k, capacity)
        out_a = expert_forward(u_rows_a, w1_a, w3_a, w2_a)[3]
        x_mid = combine(x_in, gate_a, send_back(out_a), maps_a[0])
        u_rows_b = send_rows(x_mid, maps_b[1] // top_k, capacity)
        out_b = expert_forward(u_rows_b, w1_b, w3_b, w2_b)[3]
        x_out = combine(x_mid, gate_b, send_back(out_b), maps_b[0])
        dx_mid, dgate_b, grads_b = layer_backward(dy_out, u_rows_b, gate_b, maps_b, capacity, w1_b, w3_b, w2_b)
        x_again, dx_mid = lax.optimization_barrier((x_in, dx_mid))
        u_again = send_rows(x_again, maps_a[1] // top_k, capacity)
        dx_in, dgate_a, grads_a = layer_backward(dx_mid, u_again, gate_a, maps_a, capacity, w1_a, w3_a, w2_a)
        return (x_out, dx_in) + grads_a + grads_b + (dgate_a, dgate_b)

    return jax.shard_map(device_program, mesh=mesh, in_specs=(tok_spec,) * 6 + (w_spec,) * 6, out_specs=(tok_spec,) * 10, check_vma=False)
```

profile of v0, /device:TPU:97, one launch (start us, length us, event | category | flops | bytes accessed | tf_op | source)
XLA Modules:
  0.0 2069.9 jit_solution(8523438003764498564)
XLA Ops:
  13.8 15.6 scatter_custom_fusion
  30.1 65.2 %gather_fusion = bf16[16384,256]{1,0:T(8,128)(2,1)} fusion(bf16[512,256]{1,0:T(8,128)(2,1)S(1)} %copy-done.2, s32[16384]{0:T(1024)S(1)} %get-tuple-element.67), kind=kCustom, calls=%fused_computation.clone | custom fusion | bytes 16842752 | tf_op jit(solution)/shard_map/jit(_take)/gather | solution.py:21
  105.0 113.3 %all_to_all.145 = bf16[32,512,256]{2,1,0:T(8,128)(2,1)S(1)} all-to-all(bf16[32,512,256]{2,1,0:T(8,128)(2,1)S(1)} %bitcast.253), channel_id=1, replica_groups=mesh['dp'=1,'ep'=32] {'ep'}, dimensions={0} | all-to-all | bytes 16777216 | tf_op jit(solution)/shard_map/all_to_all | solution.py:23
  237.5 15.5 copy.101
  253.4 84.5 %reduce.8 = bf16[16384,256]{1,0:T(8,128)(2,1)} reduce(bf16[16384,1,256]{2,1,0:T(2,128)(2,1)} %bitcast.247, bf16[]{:T(256)} %broadcast.272), dimensions={1}, to_apply=%bitcast.222.reduce_sub_computation | reduce | bytes 16777218
  338.0 19.8 reshape.658
  376.2 15.6 scatter_custom_fusion.1
  391.9 65.2 %gather_fusion.5 = bf16[16384,256]{1,0:T(8,128)(2,1)} fusion(bf16[512,256]{1,0:T(8,128)(2,1)S(1)} %copy-done.8, s32[16384]{0:T(1024)S(1)} %get-tuple-element.69), kind=kCustom, calls=%fused_computation.5.clone | custom fusion | bytes 16842752 | tf_op jit(solution)/shard_map/jit(_take)/gather | solution.py:21
  457.2 11.0 all-to-all-done.1
  468.2 23.4 %reshape.659 = bf16[16384,1,256]{2,1,0:T(2,128)(2,1)} reshape(bf16[32,2,65536]{2,1,0:T(2,128)(2,1)} %all-to-all-done.1) | data formatting | bytes 16777216
  491.6 10.8 copy.97
  502.5 17.5 gather_fusion.1
  523.0 65.2 %gather_fusion.2 = bf16[16384,256]{1,0:T(8,128)(2,1)} fusion(bf16[512,256]{1,0:T(8,128)(2,1)S(1)} %add_convert_fusion.3, s32[16384]{0:T(1024)S(1)} %get-tuple-element.69), kind=kCustom, calls=%fused_computation.4.clone | custom fusion | bytes 16842752 | tf_op jit(solution)/shard_map/jit(_take)/gather | solution.py:21
  598.0 114.2 %all_to_all.146 = bf16[32,512,256]{2,1,0:T(8,128)(2,1)} all-to-all(bf16[32,512,256]{2,1,0:T(8,128)(2,1)S(1)} %bitcast.256), channel_id=1, replica_groups=mesh['dp'=1,'ep'=32] {'ep'}, dimensions={0} | all-to-all | bytes 16777216 | tf_op jit(solution)/shard_map/all_to_all | solution.py:23
  717.8 90.5 %gather_fusion.4 = f32[16384]{0:T(1024)S(1)} fusion(f32[4096]{0:T(1024)S(1)} %reshape.466, s32[16384]{0:T(1024)S(1)} %get-tuple-element.68), kind=kCustom, calls=%fused_computation.2.clone | custom fusion | bytes 196608 | tf_op jit(solution)/shard_map/jit(_take)/gather | solution.py:21
  809.0 12.9 all-to-all-done.5
  821.9 12.8 all-to-all-start.4
  852.5 11.3 multiply_convert_fusion.2
  898.1 15.5 copy.100
  913.6 84.5 %reduce.10 = bf16[16384,256]{1,0:T(8,128)(2,1)} reduce(bf16[16384,1,256]{2,1,0:T(2,128)(2,1)} %bitcast.249, bf16[]{:T(256)} %broadcast.272), dimensions={1}, to_apply=%bitcast.221.reduce_sub_computation | reduce | bytes 16777218
  998.1 19.8 reshape.662
  1035.2 11.5 fusion.9
  1046.7 15.5 copy.99
  1062.2 84.5 %reduce.9 = bf16[16384,256]{1,0:T(8,128)(2,1)} reduce(bf16[16384,1,256]{2,1,0:T(2,128)(2,1)} %bitcast.250, bf16[]{:T(256)} %broadcast.272), dimensions={1}, to_apply=%bitcast.220.reduce_sub_computation | reduce | bytes 16777218
  1146.6 19.7 reshape.660
  1173.4 23.0 %gather_fusion.12 = f32[4096]{0:T(1024)S(1)} fusion(f32[16384]{0:T(1024)S(1)} %bitcast.228, s32[4096]{0:T(1024)S(1)} %copy-done.36), kind=kCustom, calls=%fused_computation.12.clone | custom fusion | bytes 49152 | tf_op jit(solution)/shard_map/jit(_take)/gather | solution.py:70
  1197.1 23.4 %reshape.663 = bf16[16384,1,256]{2,1,0:T(2,128)(2,1)} reshape(bf16[32,2,65536]{2,1,0:T(2,128)(2,1)} %all-to-all-done.3) | data formatting | bytes 16777216
  1220.5 10.8 copy.96
  1231.3 17.4 gather_fusion.3
  1248.7 29.0 %all-to-all-done.6 = bf16[32,2,65536]{2,1,0:T(2,128)(2,1)} async-done(((bf16[32,2,65536]{2,1,0:T(2,128)(2,1)}), bf16[32,2,65536]{2,1,0:T(2,128)(2,1)}, u32[]{:S(2)}, u32[]{:S(2)}) %all-to-all-start.6) | async-done | bytes 8388640 | tf_op jit(solution)/shard_map/all_to_all | solution.py:27
  1277.7 23.4 %reshape.661 = bf16[16384,1,256]{2,1,0:T(2,128)(2,1)} reshape(bf16[32,2,65536]{2,1,0:T(2,128)(2,1)} %all-to-all-done.6) | data formatting | bytes 16777216
  1312.0 20.5 gather_fusion.6
  1337.8 65.2 %gather_fusion.8 = bf16[16384,256]{1,0:T(8,128)(2,1)} fusion(bf16[512,256]{1,0:T(8,128)(2,1)S(1)} %copy-done.3, s32[16384]{0:T(1024)S(1)} %copy-done.25), kind=kCustom, calls=%fused_computation.6.clone | custom fusion | bytes 16842752 | tf_op jit(solution)/shard_map/jit(_take)/gather | solution.py:21
  1403.0 65.2 %gather_fusion.9 = bf16[16384,256]{1,0:T(8,128)(2,1)} fusion(bf16[512,256]{1,0:T(8,128)(2,1)S(1)} %add_convert_fusion.1, s32[16384]{0:T(1024)S(1)} %copy-done.25), kind=kCustom, calls=%fused_computation.7.clone | custom fusion | bytes 16842752 | tf_op jit(solution)/shard_map/jit(_take)/gather | solution.py:21
  1477.9 114.2 %all_to_all.147 = bf16[32,512,256]{2,1,0:T(8,128)(2,1)} all-to-all(bf16[32,512,256]{2,1,0:T(8,128)(2,1)S(1)} %bitcast.257), channel_id=1, replica_groups=mesh['dp'=1,'ep'=32] {'ep'}, dimensions={0} | all-to-all | bytes 16777216 | tf_op jit(solution)/shard_map/all_to_all | solution.py:23
  1597.7 90.5 %gather_fusion.7 = f32[16384]{0:T(1024)S(1)} fusion(f32[4096]{0:T(1024)S(1)} %reshape.471, s32[16384]{0:T(1024)S(1)} %copy-done.33), kind=kCustom, calls=%fused_computation.11.clone | custom fusion | bytes 196608 | tf_op jit(solution)/shard_map/jit(_take)/gather | solution.py:21
  1688.9 13.0 all-to-all-done.9
  1701.9 13.0 all-to-all-start.7
  1732.5 11.3 multiply_convert_fusion.3
  1768.9 11.5 fusion.8
  1780.4 15.5 copy.98
  1795.9 84.5 %reduce.11 = bf16[16384,256]{1,0:T(8,128)(2,1)} reduce(bf16[16384,1,256]{2,1,0:T(2,128)(2,1)} %bitcast.248, bf16[]{:T(256)} %broadcast.272), dimensions={1}, to_apply=%bitcast.219.reduce_sub_computation | reduce | bytes 16777218
  1880.4 19.8 reshape.664
  1958.1 23.0 %gather_fusion.11 = f32[4096]{0:T(1024)S(1)} fusion(f32[16384]{0:T(1024)S(1)} %bitcast.227, s32[4096]{0:T(1024)S(1)} %copy-done.35), kind=kCustom, calls=%fused_computation.3.clone | custom fusion | bytes 49152 | tf_op jit(solution)/shard_map/jit(_take)/gather | solution.py:70
  1982.0 29.5 %all-to-all-done.10 = bf16[32,2,65536]{2,1,0:T(2,128)(2,1)} async-done(((bf16[32,2,65536]{2,1,0:T(2,128)(2,1)}), bf16[32,2,65536]{2,1,0:T(2,128)(2,1)}, u32[]{:S(2)}, u32[]{:S(2)}) %all-to-all-start.10) | async-done | bytes 8388640 | tf_op jit(solution)/shard_map/all_to_all | solution.py:27
  2011.5 23.4 %reshape.665 = bf16[16384,1,256]{2,1,0:T(2,128)(2,1)} reshape(bf16[32,2,65536]{2,1,0:T(2,128)(2,1)} %all-to-all-done.10) | data formatting | bytes 16777216
  2034.9 10.8 copy.94
  2045.8 17.5 gather_fusion.10
  (198 shorter events, 297.4 us)
Async XLA Ops:
  0.6 850.9 %copy-start = (bf16[1,256,128]{2,1,0:T(8,128)(2,1)S(1)}, bf16[1,256,128]{2,1,0:T(8,128)(2,1)}, u32[]{:S(2)}) copy-start(bf16[1,256,128]{2,1,0:T(8,128)(2,1)} %param.30) | copy-start | bytes 196612
  0.7 29.5 %copy-start.2 = (bf16[512,256]{1,0:T(8,128)(2,1)S(1)}, bf16[512,256]{1,0:T(8,128)(2,1)}, u32[]{:S(2)}) copy-start(bf16[512,256]{1,0:T(8,128)(2,1)} %param.20) | copy-start | bytes 786436
  13.7 488.7 %copy-start.34 = (s32[4096]{0:T(1024)}, s32[4096]{0:T(1024)S(1)}, u32[]{:S(2)}) copy-start(s32[4096]{0:T(1024)S(1)} %get-tuple-element.76) | copy-start | bytes 49156
  29.3 66.0 %copy-start.22 = (s32[16384]{0:T(1024)}, s32[16384]{0:T(1024)S(1)}, u32[]{:S(2)}) copy-start(s32[16384]{0:T(1024)S(1)} %scatter_custom_fusion) | copy-start | bytes 196612
  29.4 65.9 %copy-start.37 = (pred[16384]{0:T(1024)(128)(4,1)}, pred[16384]{0:T(1024)(128)(4,1)S(1)}, u32[]{:S(2)}) copy-start(pred[16384]{0:T(1024)(128)(4,1)S(1)} %compare_and_fusion.1) | copy-start | bytes 49156
  30.1 65.2 %copy-start.24 = (s32[16384]{0:T(1024)}, s32[16384]{0:T(1024)S(1)}, u32[]{:S(2)}) copy-start(s32[16384]{0:T(1024)S(1)} %get-tuple-element.67) | copy-start | bytes 196612
  104.9 116.6 %copy-start.27 = (bf16[1,256,128]{2,1,0:T(8,128)(2,1)S(1)}, bf16[1,256,128]{2,1,0:T(8,128)(2,1)}, u32[]{:S(2)}) copy-start(bf16[1,256,128]{2,1,0:T(8,128)(2,1)} %param.26) | copy-start | bytes 196612
  357.8 34.1 %copy-start.8 = (bf16[512,256]{1,0:T(8,128)(2,1)S(1)}, bf16[512,256]{1,0:T(8,128)(2,1)}, u32[]{:S(2)}) copy-start(bf16[512,256]{1,0:T(8,128)(2,1)} %param.25) | copy-start | bytes 786436
  357.8 110.4 %all-to-all-start.1 = ((bf16[32,2,65536]{2,1,0:T(2,128)(2,1)}), bf16[32,2,65536]{2,1,0:T(2,128)(2,1)}, u32[]{:S(2)}, u32[]{:S(2)}) async-start(bf16[32,2,65536]{2,1,0:T(2,128)(2,1)} %reshape.658), calls=%async_computation.1 | async-start | bytes 16777216 | tf_op jit(solution)/shard_map/all_to_all | solution.py:27
  364.1 93.0 %copy-start.31 = (s32[4096]{0:T(1024)}, s32[4096]{0:T(1024)S(1)}, u32[]{:S(2)}) copy-start(s32[4096]{0:T(1024)S(1)} %eq.58) | copy-start | bytes 49156
  364.7 155.2 %copy-start.19 = (f32[512,8]{1,0:T(8,128)}, f32[512,8]{1,0:T(8,128)S(1)}, u32[]{:S(2)}) copy-start(f32[512,8]{1,0:T(8,128)S(1)} %copy.52) | copy-start | bytes 49156
  457.1 62.9 %copy-start.46 = (pred[4096]{0:T(1024)(128)(4,1)}, pred[4096]{0:T(1024)(128)(4,1)S(1)}, u32[]{:S(2)}) copy-start(pred[4096]{0:T(1024)(128)(4,1)S(1)} %compare_and_fusion.3) | copy-start | bytes 12292
  523.0 65.2 %copy-start.6 = (bf16[512,256]{1,0:T(8,128)(2,1)}, bf16[512,256]{1,0:T(8,128)(2,1)S(1)}, u32[]{:S(2)}) copy-start(bf16[512,256]{1,0:T(8,128)(2,1)S(1)} %add_convert_fusion.3) | copy-start | bytes 786436
  712.2 109.7 %all-to-all-start.5 = ((bf16[32,512,256]{2,1,0:T(8,128)(2,1)}), bf16[32,512,256]{2,1,0:T(8,128)(2,1)}, u32[]{:S(2)}, u32[]{:S(2)}) async-start(bf16[32,512,256]{2,1,0:T(8,128)(2,1)} %bitcast.254), calls=%async_computation.5 | async-start | bytes 16777216 | tf_op jit(solution)/shard_map/all_to_all | solution.py:23
  717.7 90.7 %copy-start.17 = (f32[512,8]{1,0:T(8,128)}, f32[512,8]{1,0:T(8,128)S(1)}, u32[]{:S(2)}) copy-start(f32[512,8]{1,0:T(8,128)S(1)} %copy.57) | copy-start | bytes 49156
  717.8 116.9 %copy-start.26 = (bf16[1,256,128]{2,1,0:T(8,128)(2,1)S(1)}, bf16[1,256,128]{2,1,0:T(8,128)(2,1)}, u32[]{:S(2)}) copy-start(bf16[1,256,128]{2,1,0:T(8,128)(2,1)} %param.29) | copy-start | bytes 196612
  821.9 21.9 %all-to-all-start.4 = ((f32[32,1,512]{2,1,0:T(1,128)}), f32[32,1,512]{2,1,0:T(1,128)S(1)}, u32[]{:S(2)}, u32[]{:S(2)}) async-start(f32[32,1,512]{2,1,0:T(1,128)} %bitcast.20), calls=%async_computation.4 | async-start | bytes 131072 | tf_op jit(solution)/shard_map/all_to_all | solution.py:23
  834.8 9.1 copy-start.41
  843.8 8.7 copy-start.10
  871.6 146.3 %all-to-all-start.12 = ((f32[1,32,512]{2,0,1:T(1,128)}), f32[1,32,512]{2,0,1:T(1,128)S(1)}, u32[]{:S(2)}, u32[]{:S(2)}) async-start(f32[1,32,512]{2,0,1:T(1,128)} %bitcast.49), calls=%async_computation.12 | async-start | bytes 131072 | tf_op jit(solution)/shard_map/all_to_all | solution.py:27
  1017.9 148.5 %all-to-all-start.3 = ((bf16[32,2,65536]{2,1,0:T(2,128)(2,1)}), bf16[32,2,65536]{2,1,0:T(2,128)(2,1)}, u32[]{:S(2)}, u32[]{:S(2)}) async-start(bf16[32,2,65536]{2,1,0:T(2,128)(2,1)} %reshape.662), calls=%async_computation.3 | async-start | bytes 16777216 | tf_op jit(solution)/shard_map/all_to_all | solution.py:27
  1024.8 10.4 copy-start.12
  1166.4 111.4 %all-to-all-start.6 = ((bf16[32,2,65536]{2,1,0:T(2,128)(2,1)}), bf16[32,2,65536]{2,1,0:T(2,128)(2,1)}, u32[]{:S(2)}, u32[]{:S(2)}) async-start(bf16[32,2,65536]{2,1,0:T(2,128)(2,1)} %reshape.660), calls=%async_computation.6 | async-start | bytes 16777216 | tf_op jit(solution)/shard_map/all_to_all | solution.py:27
  1173.4 23.1 %copy-start.32 = (s32[4096]{0:T(1024)S(1)}, s32[4096]{0:T(1024)}, u32[]{:S(2)}) copy-start(s32[4096]{0:T(1024)} %copy-done.31) | copy-start | bytes 49156
  1173.4 23.1 %copy-start.40 = (s32[4096]{0:T(1024)S(1)}, s32[4096]{0:T(1024)}, u32[]{:S(2)}) copy-start(s32[4096]{0:T(1024)} %copy-done.39) | copy-start | bytes 49156
  1312.0 20.5 copy-start.18
  1312.0 25.7 %copy-start.9 = (bf16[512,256]{1,0:T(8,128)(2,1)S(1)}, bf16[512,256]{1,0:T(8,128)(2,1)}, u32[]{:S(2)}) copy-start(bf16[512,256]{1,0:T(8,128)(2,1)} %param.25) | copy-start | bytes 786436
  1312.0 25.8 %copy-start.3 = (bf16[512,256]{1,0:T(8,128)(2,1)S(1)}, bf16[512,256]{1,0:T(8,128)(2,1)}, u32[]{:S(2)}) copy-start(bf16[512,256]{1,0:T(8,128)(2,1)} %param.20) | copy-start | bytes 786436
  1312.0 25.8 %copy-start.25 = (s32[16384]{0:T(1024)S(1)}, s32[16384]{0:T(1024)}, u32[]{:S(2)}) copy-start(s32[16384]{0:T(1024)} %copy-done.24) | copy-start | bytes 196612
  1337.8 65.2 %copy-start.4 = (bf16[512,256]{1,0:T(8,128)(2,1)}, bf16[512,256]{1,0:T(8,128)(2,1)S(1)}, u32[]{:S(2)}) copy-start(bf16[512,256]{1,0:T(8,128)(2,1)S(1)} %add_convert_fusion.1) | copy-start | bytes 786436
  1403.0 65.2 %copy-start.38 = (pred[16384]{0:T(1024)(128)(4,1)S(1)}, pred[16384]{0:T(1024)(128)(4,1)}, u32[]{:S(2)}) copy-start(pred[16384]{0:T(1024)(128)(4,1)} %copy-done.37) | copy-start | bytes 49156
  1592.2 109.7 %all-to-all-start.9 = ((bf16[32,512,256]{2,1,0:T(8,128)(2,1)}), bf16[32,512,256]{2,1,0:T(8,128)(2,1)}, u32[]{:S(2)}, u32[]{:S(2)}) async-start(bf16[32,512,256]{2,1,0:T(8,128)(2,1)} %bitcast.255), calls=%async_computation.9 | async-start | bytes 16777216 | tf_op jit(solution)/shard_map/all_to_all | solution.py:23
  1597.7 90.6 %copy-start.23 = (s32[16384]{0:T(1024)S(1)}, s32[16384]{0:T(1024)}, u32[]{:S(2)}) copy-start(s32[16384]{0:T(1024)} %copy-done.22) | copy-start | bytes 196612
  1597.7 117.2 %copy-start.28 = (bf16[1,256,128]{2,1,0:T(8,128)(2,1)S(1)}, bf16[1,256,128]{2,1,0:T(8,128)(2,1)}, u32[]{:S(2)}) copy-start(bf16[1,256,128]{2,1,0:T(8,128)(2,1)} %param.26) | copy-start | bytes 196612
  1701.9 22.0 %all-to-all-start.7 = ((f32[32,1,512]{2,1,0:T(1,128)}), f32[32,1,512]{2,1,0:T(1,128)S(1)}, u32[]{:S(2)}, u32[]{:S(2)}) async-start(f32[32,1,512]{2,1,0:T(1,128)} %bitcast.29), calls=%async_computation.7 | async-start | bytes 131072 | tf_op jit(solution)/shard_map/all_to_all | solution.py:23
  1714.9 9.0 copy-start.43
  1723.9 8.6 copy-start.11
  1723.9 8.6 copy-start.45
  1751.6 148.6 %all-to-all-start.11 = ((f32[1,32,512]{2,0,1:T(1,128)}), f32[1,32,512]{2,0,1:T(1,128)S(1)}, u32[]{:S(2)}, u32[]{:S(2)}) async-start(f32[1,32,512]{2,0,1:T(1,128)} %bitcast.46), calls=%async_computation.11 | async-start | bytes 131072 | tf_op jit(solution)/shard_map/all_to_all | solution.py:27
  1758.5 10.4 copy-start.14
  1900.2 111.4 %all-to-all-start.10 = ((bf16[32,2,65536]{2,1,0:T(2,128)(2,1)}), bf16[32,2,65536]{2,1,0:T(2,128)(2,1)}, u32[]{:S(2)}, u32[]{:S(2)}) async-start(bf16[32,2,65536]{2,1,0:T(2,128)(2,1)} %reshape.664), calls=%async_computation.10 | async-start | bytes 16777216 | tf_op jit(solution)/shard_map/all_to_all | solution.py:27
  1921.6 10.1 copy-start.48
  1921.6 11.0 copy-start.7
  1921.6 11.0 copy-start.21
  1947.8 10.3 copy-start.35
  1958.1 23.0 %copy-start.47 = (pred[4096]{0:T(1024)(128)(4,1)S(1)}, pred[4096]{0:T(1024)(128)(4,1)}, u32[]{:S(2)}) copy-start(pred[4096]{0:T(1024)(128)(4,1)} %copy-done.46) | copy-start | bytes 12292
  2045.8 23.9 %copy-start.1 = (bf16[1,256,128]{2,1,0:T(8,128)(2,1)S(1)}, bf16[1,256,128]{2,1,0:T(8,128)(2,1)}, u32[]{:S(2)}) copy-start(bf16[1,256,128]{2,1,0:T(8,128)(2,1)} %param.30) | copy-start | bytes 196612
  2045.8 23.1 %copy-start.5 = (bf16[512,256]{1,0:T(8,128)(2,1)S(1)}, bf16[512,256]{1,0:T(8,128)(2,1)}, u32[]{:S(2)}) copy-start(bf16[512,256]{1,0:T(8,128)(2,1)} %copy-done.4) | copy-start | bytes 786436
  (16 other events, 94.5 us)
where the time goes:
time: 2090 us; the launch traced here: 2070 us
  local copies, waits for them, and re-layouts  947 us (45%)
  other arithmetic  407 us (19%)
  blocking collectives  342 us (16%)
  matrix products  200 us (10%)
  waiting for transfers between devices  95.5 us (5%)
  starting transfers between devices  77.3 us (4%)
    gather x7, local copies, waits for them, and re-layouts, send_rows(): send_buf = jnp.take(rows, index, axis=0, mode='fill', fill_value=0)  507 us
    all_to_all x3, blocking collectives, send_rows(): return lax.all_to_all(send_buf, 'ep', 0, 1, tiled=True)  342 us
    unnamed x4, other arithmetic  338 us
    unnamed x127, local copies, waits for them, and re-layouts  224 us
    all_to_all x6, waiting for transfers between devices, send_back(): back_rows = lax.all_to_all(rows, 'ep', 1, 0, tiled=True)  69.6 us
    gather x2, local copies, waits for them, and re-layouts, layer_backward(): jnp.take(send_back(dgate_rows), pair_row, axis=0).reshape(tok_dev, top_k)  46.1 us
  transfers between devices with their start and end apart: 10, of which 5 were waited for; matrix products, arithmetic and copies ran while one was open for 42% of the time, Pallas kernels for 0%

commit v1 on v0

v1 whole, which is shorter than its diff:
```python
import functools

import jax
import jax.numpy as jnp
from jax import lax
from jax.experimental import pallas as pl
from jax.experimental.pallas import tpu as pltpu
from jax.sharding import PartitionSpec as P

F32 = jnp.float32
BF16 = jnp.bfloat16


def mm(a, b, ca, cb):
    return lax.dot_general(a, b, (((ca,), (cb,)), ((), ())), preferred_element_type=F32)


def route(expert, idx_t, gate_t):
    picked = idx_t == expert
    gate = jnp.sum(jnp.where(picked, gate_t, 0.0), axis=0, keepdims=True)
    count = jnp.sum(jnp.where(picked, 1.0, 0.0), axis=0, keepdims=True)
    return picked, gate, count > 0.5


def expert_in(w, x_t, mask):
    d = x_t.shape[0]
    ab = mm(jnp.concatenate([w[:d], w[d : 2 * d]], axis=1), x_t, 0, 0)
    ab = jnp.where(mask, ab, 0.0)
    f = w.shape[1]
    return ab[:f], ab[f:]


def down(w, d):
    return jnp.concatenate([w[2 * d : 2 * d + d // 2], w[2 * d + d // 2 :]], axis=1)


def expert_forward(w, x_t, mask):
    d = x_t.shape[0]
    a, b = expert_in(w, x_t, mask)
    s = jax.nn.sigmoid(a)
    silu = a * s
    h = (silu * b).astype(BF16)
    o = mm(down(w, d), h, 0, 0).astype(BF16)
    return a, b, s, silu, h, o


def expert_backward(w, x, dy_t, gate, a, b, s, silu, h, o):
    d = x.shape[1]
    dy = dy_t.astype(F32)
    dgate = jnp.sum(dy * o.astype(F32), axis=0, keepdims=True)
    q = (gate * dy).astype(BF16)
    dh = mm(down(w, d), q, 1, 0)
    dw2 = mm(h, q, 1, 1)
    da = (dh * b * s * (1.0 + a * (1.0 - s))).astype(BF16)
    db = (dh * silu).astype(BF16)
    dab = jnp.concatenate([da, db], axis=0)
    dw13_t = mm(dab, x, 1, 0)
    du = mm(jnp.concatenate([w[:d], w[d : 2 * d]], axis=1), dab, 1, 0).astype(BF16)
    return dgate, dw13_t, dw2, du


def forward_kernel(x_ref, idx_ref, gate_ref, w_ref, y_ref, xt_s, acc_s):
    xt_s[...] = x_ref[...].T
    acc_s[...] = xt_s[...].astype(F32)

    def body(e, carry):
        picked, gate, mask = route(e, idx_ref[...], gate_ref[...])
        o = expert_forward(w_ref[e], xt_s[...], mask)[5]
        acc_s[...] += gate * o.astype(F32)
        return carry

    lax.fori_loop(0, w_ref.shape[0], body, 0)
    y_ref[...] = acc_s[...].astype(BF16).T


def both_kernel(fwd, x_ref, dy_ref, idx_ref, gate_ref, w_ref, *refs):
    if fwd:
        y_ref, dx_ref, dg_ref, dw_ref, xt_s, dyt_s, dx_s, acc_s = refs
    else:
        dx_ref, dg_ref, dw_ref, xt_s, dyt_s, dx_s = refs
    d = x_ref.shape[1]
    xt_s[...] = x_ref[...].T
    dyt_s[...] = dy_ref[...].T
    dx_s[...] = dyt_s[...].astype(F32)
    if fwd:
        acc_s[...] = xt_s[...].astype(F32)
    dg_ref[...] = jnp.zeros_like(dg_ref)

    def body(e, carry):
        picked, gate, mask = route(e, idx_ref[...], gate_ref[...])
        parts = expert_forward(w_ref[e], xt_s[...], mask)
        if fwd:
            acc_s[...] += gate * parts[5].astype(F32)
        dgate, dw13_t, dw2, du = expert_backward(w_ref[e], x_ref[...], dyt_s[...], gate, *parts)
        dg_ref[...] += jnp.where(picked, dgate, 0.0)
        dw_ref[e, : 2 * w_ref.shape[2]] = dw13_t
        dw_ref[e, 2 * w_ref.shape[2] :] = dw2
        dx_s[...] += du.astype(F32)
        return carry

    lax.fori_loop(0, w_ref.shape[0], body, 0)
    dx_ref[...] = dx_s[...].astype(BF16).T
    if fwd:
        y_ref[...] = acc_s[...].astype(BF16).T


def call(kernel, outs, scratch, *args):
    vmem = pl.BlockSpec(memory_space=pltpu.VMEM)
    return pl.pallas_call(
        kernel,
        out_shape=outs,
        in_specs=[vmem] * len(args),
        out_specs=jax.tree.map(lambda _: vmem, outs),
        scratch_shapes=scratch,
        compiler_params=pltpu.CompilerParams(vmem_limit_bytes=48 * 2**20),
    )(*args)


def pack(w1, w3, w2):
    half = w2.shape[2] // 2
    return jnp.concatenate([w1[0], w3[0], w2[0, :, :half], w2[0, :, half:]], axis=0)


def unpack(dw, f):
    return dw[:, :f].transpose(0, 2, 1), dw[:, f : 2 * f].transpose(0, 2, 1), dw[:, 2 * f :]


def solution(mesh):
    tok_spec = P(("dp", "ep"))
    w_spec = P("ep")

    def device_program(x_in, idx_a, idx_b, gate_a, gate_b, dy_out, w1_a, w3_a, w2_a, w1_b, w3_b, w2_b):
        (tok, d), f = x_in.shape, w1_a.shape[2]
        w_a = lax.all_gather(pack(w1_a, w3_a, w2_a), "ep")
        w_b = lax.all_gather(pack(w1_b, w3_b, w2_b), "ep")
        n = w_a.shape[0]
        rows = jax.ShapeDtypeStruct((tok, d), BF16)
        dgs = jax.ShapeDtypeStruct((idx_a.shape[1], tok), F32)
        dws = jax.ShapeDtypeStruct((n, 2 * f + f, d), F32)
        xt, acc = pltpu.VMEM((d, tok), BF16), pltpu.VMEM((d, tok), F32)
        x_mid = call(forward_kernel, rows, [xt, acc], x_in, idx_a.T, gate_a.T, w_a)
        x_out, dx_mid, dg_b, dw_b = call(
            functools.partial(both_kernel, True), (rows, rows, dgs, dws), [xt, xt, acc, acc],
            x_mid, dy_out, idx_b.T, gate_b.T, w_b)
        dx_in, dg_a, dw_a = call(
            functools.partial(both_kernel, False), (rows, dgs, dws), [xt, xt, acc],
            x_in, dx_mid, idx_a.T, gate_a.T, w_a)
        dw_b = lax.psum_scatter(dw_b, "ep", scatter_dimension=0, tiled=True)
        dw_a = lax.psum_scatter(dw_a, "ep", scatter_dimension=0, tiled=True)
        return (x_out, dx_in) + unpack(dw_a, f) + unpack(dw_b, f) + (dg_a.T, dg_b.T)

    return jax.shard_map(device_program, mesh=mesh, in_specs=(tok_spec,) * 6 + (w_spec,) * 6, out_specs=(tok_spec,) * 10, check_vma=False)
```

time: 2090 us -> 347 us (0.17)
  local copies, waits for them, and re-layouts: 947 us -> 12.8 us
  other arithmetic: 407 us -> 3.12 us
  blocking collectives: 342 us -> 0 us
  matrix products: 200 us -> 0 us
  waiting for transfers between devices: 95.5 us -> 225 us
  Pallas kernels: 0 us -> 90.4 us
  starting transfers between devices: 77.3 us -> 0.26 us
    gather x13 -> x0, local copies, waits for them, and re-layouts: 626 us -> none  [the longest x7 507 us: send_rows(): send_buf = jnp.take(rows, index, axis=0, mode='fill', fill_value=0)]
    all_to_all x3 -> x0, blocking collectives: 342 us -> none  [send_rows(): return lax.all_to_all(send_buf, 'ep', 0, 1, tiled=True)]
    unnamed x4 -> x0, other arithmetic: 338 us -> none
    unnamed x127 -> x22, local copies, waits for them, and re-layouts: 224 us -> 7.79 us
    dot_general x22 -> x0, matrix products: 200 us -> none  [the longest x4 36.3 us: expert_forward(): jnp.einsum('erf,efd->erd', hidden, w_down, preferred_element_type=jnp.flo...]
    reduce_scatter x0 -> x2, waiting for transfers between devices: none -> 153 us  [the longest x1 96.3 us: device_program(): dw_a = lax.psum_scatter(dw_a, 'ep', scatter_dimension=0, tiled=True)]
    all_to_all x10 -> x0, waiting for transfers between devices: 95.5 us -> none  [the longest x6 69.6 us: send_back(): back_rows = lax.all_to_all(rows, 'ep', 1, 0, tiled=True)]
    pallas_call x0 -> x3, Pallas kernels: none -> 90.4 us  [call(): pl.pallas_call(kernel, out_shape=outs, in_specs=[vmem] * len(args), out_s...]
  transfers between devices with their start and end apart: 10 -> 4, of which waited for: 5 -> 4; matrix products, arithmetic and copies ran while one was open for 42% -> 2% of each run, Pallas kernels for 0% -> 15%
where the time goes in v1:
time: 347 us; the launch traced here: 346 us
  waiting for transfers between devices  225 us (65%)
  Pallas kernels  90.4 us (26%)
  between operations  13.8 us (4%)
  local copies, waits for them, and re-layouts  12.8 us (4%)
    reduce_scatter x1, waiting for transfers between devices, device_program(): dw_a = lax.psum_scatter(dw_a, 'ep', scatter_dimension=0, tiled=True)  96.3 us
    pallas_call x3, Pallas kernels, call(): pl.pallas_call(kernel, out_shape=outs, in_specs=[vmem] * len(args), out_s...  90.4 us
    reduce_scatter x1, waiting for transfers between devices, device_program(): dw_b = lax.psum_scatter(dw_b, 'ep', scatter_dimension=0, tiled=True)  57 us
    all_gather x1, waiting for transfers between devices, device_program(): w_a = lax.all_gather(pack(w1_a, w3_a, w2_a), 'ep')  46.6 us
    all_gather x1, waiting for transfers between devices, device_program(): w_b = lax.all_gather(pack(w1_b, w3_b, w2_b), 'ep')  25.4 us
    unnamed x22, local copies, waits for them, and re-layouts  7.79 us
  transfers between devices with their start and end apart: 4, of which 4 were waited for; matrix products, arithmetic and copies ran while one was open for 2% of the time, Pallas kernels for 15%

profile of v1, /device:TPU:97, one launch (start us, length us, event | category | flops | bytes accessed | tf_op | source)
XLA Modules:
  0.0 345.8 jit_solution(4578205865062603748)
XLA Ops:
  7.2 0.1 all-gather.5.cloned.1.call-start
  7.3 0.8 slice_bitcast_fusion.7
  8.0 1.6 pad_maximum_fusion
  9.6 0.1 all-gather.5.cloned.1.call-update
  9.7 0.1 all-gather.7.cloned.1.call-start
  9.7 0.8 slice_bitcast_fusion.5
  10.5 1.6 pad_maximum_fusion.1
  12.1 0.1 all-gather.7.cloned.1.call-update
  12.1 0.1 reduce-scatter.5.cloned.1.call-start
  12.2 46.6 %all-gather.5.cloned.1.call-done = bf16[24576,128]{1,0:T(8,128)(2,1)} async-done(((bf16[768,128]{1,0:T(8,128)(2,1)}), bf16[24576,128]{1,0:T(8,128)(2,1)}) %all-gather.5.cloned.1.call-update) | async-done | bytes 6291472 | tf_op jit(solution)/shard_map/all_gather | solution.py:134
  58.8 0.0 copy-start
  58.8 0.9 copy-done
  59.7 0.0 copy-start.3
  59.7 0.7 copy-done.3
  60.4 0.0 copy-start.5
  60.4 0.7 copy-done.5
  61.2 0.0 copy-start.1
  61.2 0.0 copy-start.4
  61.2 0.0 copy-start.6
  61.2 17.5 %shard_map.195.x_ref = bf16[512,256]{1,0:T(8,128)(2,1)S(1)} custom-call(bf16[512,256]{1,0:T(8,128)(2,1)S(1)} %copy-done, s32[8,512]{1,0:T(8,128)S(1)} %bitcast.28, f32[8,512]{1,0:T(8,128)S(1)} %bitcast.30, bf16[32,768,128]{2,1,0:T(8,128)(2,1)} %bitcast.34), custom_call_target="tpu_custom_call" | custom-call | tf_op jit(solution)/shard_map/pallas_call | solution.py:109
  78.6 25.4 %all-gather.7.cloned.1.call-done = bf16[24576,128]{1,0:T(8,128)(2,1)} async-done(((bf16[768,128]{1,0:T(8,128)(2,1)}), bf16[24576,128]{1,0:T(8,128)(2,1)}) %all-gather.7.cloned.1.call-update) | async-done | bytes 6291472 | tf_op jit(solution)/shard_map/all_gather | solution.py:135
  104.0 0.0 copy-start.2
  104.0 0.9 copy-done.2
  105.0 0.0 copy-start.7
  105.0 0.7 copy-done.7
  105.7 0.0 copy-start.8
  105.7 0.7 copy-done.8
  106.4 37.0 %shard_map.196 = (bf16[512,256]{1,0:T(8,128)(2,1)}, bf16[512,256]{1,0:T(8,128)(2,1)S(1)}, f32[8,512]{1,0:T(8,128)}, f32[32,384,256]{2,1,0:T(8,128)}) custom-call(bf16[512,256]{1,0:T(8,128)(2,1)S(1)} %shard_map.195.x_ref, bf16[512,256]{1,0:T(8,128)(2,1)S(1)} %copy-done.2, s32[8,512]{1,0:T(8,128)S(1)} %bitcast.32, f32[8,512]{1,0:T(8,128)S(1)} %bitcast.33, ...), custom_call_target="tpu_custom_call" | custom-call | tf_op jit(solution)/shard_map/pallas_call | solution.py:109
  143.4 0.1 reduce-scatter.5.cloned.1.call-update
  143.5 0.1 reduce-scatter.3.cloned.1.call-start
  143.6 0.0 copy-done.1
  143.6 0.0 copy-done.4
  143.6 0.0 copy-done.6
  143.6 35.9 %shard_map.197 = (bf16[512,256]{1,0:T(8,128)(2,1)}, f32[8,512]{1,0:T(8,128)}, f32[32,384,256]{2,1,0:T(8,128)}) custom-call(bf16[512,256]{1,0:T(8,128)(2,1)S(1)} %copy-done.1, bf16[512,256]{1,0:T(8,128)(2,1)S(1)} %get-tuple-element.18.dy_ref, s32[8,512]{1,0:T(8,128)S(1)} %bitcast.29, f32[8,512]{1,0:T(8,128)S(1)} %bitcast.31, bf16[32,768,128]{2,1,0:T(8,128)(2,1)} %bitcast.35), custom_call_target="tpu_custom_call" | custom-call | tf_op jit(solution)/shard_map/pallas_call | solution.py:109
  179.5 0.1 reduce-scatter.3.cloned.1.call-update
  179.5 57.0 %reduce-scatter.5.cloned.1.call-done = f32[1,384,256]{2,1,0:T(8,128)} async-done(((f32[32,384,256]{2,1,0:T(8,128)}), f32[1,384,256]{2,1,0:T(8,128)}) %reduce-scatter.5.cloned.1.call-update) | async-done | bytes 393232 | tf_op jit(solution)/shard_map/reduce_scatter | solution.py:148
  236.5 1.7 fusion
  238.2 0.8 copy.25
  239.0 0.8 copy.24
  239.8 96.3 %reduce-scatter.3.cloned.1.call-done = f32[1,384,256]{2,1,0:T(8,128)} async-done(((f32[32,384,256]{2,1,0:T(8,128)}), f32[1,384,256]{2,1,0:T(8,128)}) %reduce-scatter.3.cloned.1.call-update) | async-done | bytes 393232 | tf_op jit(solution)/shard_map/reduce_scatter | solution.py:149
  336.0 1.7 fusion.1
  337.7 0.8 copy.23
  338.5 0.8 copy.22
Async XLA Ops:
  7.2 51.6 %all-gather.5.cloned.1.call-start = ((), (), s32[]{:S(2)}) async-start(), calls=%async_computation.4 | async-start | bytes 6488064 | tf_op jit(solution)/shard_map/all_gather | solution.py:134
  9.7 94.3 %all-gather.7.cloned.1.call-start = ((), (), s32[]{:S(2)}) async-start(), calls=%async_computation.5 | async-start | bytes 6488064 | tf_op jit(solution)/shard_map/all_gather | solution.py:135
  12.1 224.4 %reduce-scatter.5.cloned.1.call-start = ((), (), s32[]{:S(2)}) async-start(), calls=%async_computation.3 | async-start | bytes 12976128 | tf_op jit(solution)/shard_map/reduce_scatter | solution.py:148
  58.8 0.9 copy-start
  59.7 0.7 copy-start.3
  60.4 0.7 copy-start.5
  61.2 82.4 %copy-start.1 = (bf16[512,256]{1,0:T(8,128)(2,1)S(1)}, bf16[512,256]{1,0:T(8,128)(2,1)}, u32[]{:S(2)}) copy-start(bf16[512,256]{1,0:T(8,128)(2,1)} %x_ref.3) | copy-start | bytes 786436
  61.2 82.4 %copy-start.4 = (s32[512,8]{0,1:T(8,128)S(1)}, s32[512,8]{0,1:T(8,128)}, u32[]{:S(2)}) copy-start(s32[512,8]{0,1:T(8,128)} %param.13) | copy-start | bytes 49156
  61.2 82.4 %copy-start.6 = (f32[512,8]{0,1:T(8,128)S(1)}, f32[512,8]{0,1:T(8,128)}, u32[]{:S(2)}) copy-start(f32[512,8]{0,1:T(8,128)} %param.15) | copy-start | bytes 49156
  104.0 0.9 copy-start.2
  105.0 0.7 copy-start.7
  105.7 0.7 copy-start.8
  143.5 192.5 %reduce-scatter.3.cloned.1.call-start = ((), (), s32[]{:S(2)}) async-start(), calls=%async_computation.2 | async-start | bytes 12976128 | tf_op jit(solution)/shard_map/reduce_scatter | solution.py:149
Sparse Core Ops, SparseCore 0:
  10.7 48.0 all-gather.4
  61.4 42.5 all-gather.6
  143.6 92.8 reduce-scatter.4
  240.1 95.8 reduce-scatter.2

commit v2 on v1

v2 whole, which is shorter than its diff:
```python
import functools
import math

import jax
import jax.numpy as jnp
from jax import lax
from jax.experimental import pallas as pl
from jax.experimental.pallas import tpu as pltpu
from jax.sharding import PartitionSpec as P

F32 = jnp.float32
BF16 = jnp.bfloat16
MESH = pl.DeviceIdType.MESH


def mm(a, b, ca, cb):
    return lax.dot_general(a, b, (((ca,), (cb,)), ((), ())), preferred_element_type=F32)


def route(expert, idx_t, gate_t):
    picked = idx_t == expert
    gate = jnp.sum(jnp.where(picked, gate_t, 0.0), axis=0, keepdims=True)
    count = jnp.sum(jnp.where(picked, 1.0, 0.0), axis=0, keepdims=True)
    return picked, gate, count > 0.5


def expert_in(w, x_t, mask):
    d = x_t.shape[0]
    ab = mm(jnp.concatenate([w[:d], w[d : 2 * d]], axis=1), x_t, 0, 0)
    ab = jnp.where(mask, ab, 0.0)
    f = w.shape[1]
    return ab[:f], ab[f:]


def down(w, d):
    return jnp.concatenate([w[2 * d : 2 * d + d // 2], w[2 * d + d // 2 :]], axis=1)


def expert_forward(w, x_t, mask):
    d = x_t.shape[0]
    a, b = expert_in(w, x_t, mask)
    s = jax.nn.sigmoid(a)
    silu = a * s
    h = (silu * b).astype(BF16)
    o = mm(down(w, d), h, 0, 0).astype(BF16)
    return a, b, s, silu, h, o


def expert_backward(w, x, dy_t, gate, a, b, s, silu, h, o):
    d = x.shape[1]
    dy = dy_t.astype(F32)
    dgate = jnp.sum(dy * o.astype(F32), axis=0, keepdims=True)
    q = (gate * dy).astype(BF16)
    dh = mm(down(w, d), q, 1, 0)
    dw2 = mm(h, q, 1, 1)
    da = (dh * b * s * (1.0 + a * (1.0 - s))).astype(BF16)
    db = (dh * silu).astype(BF16)
    dab = jnp.concatenate([da, db], axis=0)
    dw13_t = mm(dab, x, 1, 0)
    du = mm(jnp.concatenate([w[:d], w[d : 2 * d]], axis=1), dab, 1, 0).astype(BF16)
    return dgate, dw13_t, dw2, du


def near_order(g):
    return g + lax.div(g, 2) * (1 - 2 * lax.rem(g, 2))


def far_order(g):
    return 2 - g + lax.div(g, 2) * (3 - 2 * lax.rem(g, 2))


def step_kernel(side, x_ref, dy_ref, ia_ref, ib_ref, ga_ref, gb_ref, w1a, w3a, w2a, w1b, w3b, w2b,
                xo_ref, dxi_ref, dw1a, dw3a, dw2a, dw1b, dw3b, dw2b, dga_ref, dgb_ref,
                wb, dwo, dws, rb, ah, af, bh, bf, xt, xm, xmt, dyt, acc, dxs,
                load_sem, ag_send, ag_recv, ag_pair, d_send, d_recv, pa_send, ah_recv, af_recv, pb_send, bh_recv, bf_recv):
    me = lax.axis_index("ep")
    core, chip = lax.rem(me, 2), lax.div(me, 2)
    cx, cy = lax.rem(chip, side), lax.div(chip, side)
    p = cx * (1 - core) + cy * core
    r = cy * (1 - core) + cx * core
    tok, d = x_ref.shape
    f = w1a.shape[2]
    wrows, grows = wb.shape[2], dwo.shape[2]
    wh, gh = wrows // 2, grows // 2
    steps = side * side
    ring = dws.shape[0]

    def member(i, j, c):
        return ((j * (1 - c) + i * c) * side + i * (1 - c) + j * c) * 2 + c

    def at(di, dj):
        return member(lax.rem(p + di, side), lax.rem(r + dj, side), core)

    sib = me + 1 - 2 * core
    first = {1: at(1, 0), -1: at(side - 1, 0)}
    second = {1: at(0, 1), -1: at(0, side - 1)}

    def rdma(src, dst, send, recv, dev):
        return pltpu.make_async_remote_copy(src_ref=src, dst_ref=dst, send_sem=send, recv_sem=recv, device_id={"ep": dev}, device_id_type=MESH)

    loads = []
    for layer, (w1, w3, w2) in enumerate(((w1a, w3a, w2a), (w1b, w3b, w2b))):
        parts = (w1.at[0], w3.at[0], w2.at[0, :, pl.ds(0, d // 2)], w2.at[0, :, pl.ds(d // 2, d // 2)])
        row = 0
        for n, part in enumerate(parts):
            loads.append(pltpu.make_async_copy(part, wb.at[layer, me, pl.ds(row, part.shape[0])], load_sem.at[4 * layer + n]))
            row += part.shape[0]
    for copy in loads:
        copy.start()

    barrier = pltpu.get_barrier_semaphore()
    for dev in (sib, *first.values(), *second.values()):
        pl.semaphore_signal(barrier, inc=1, device_id={"ep": dev}, device_id_type=MESH)
    pl.semaphore_wait(barrier, 5)

    ag_slots = []

    def ag_copy(layer, e, half, dev, pair=False):
        view = wb.at[layer, e] if half is None else wb.at[layer, e, pl.ds(half * wh, wh)]
        recv = ag_pair.at[layer, e] if pair else ag_recv.at[layer, e, half or 0]
        copy = rdma(view, view, ag_send.at[len(ag_slots)], recv, dev)
        ag_slots.append(half)
        copy.start()

    def ag_wait(layer, e, half):
        view = wb.at[layer, e] if half is None else wb.at[layer, e, pl.ds(half * wh, wh)]
        rdma(view, view, ag_send.at[0], ag_recv.at[layer, e, half or 0], me).wait_recv()

    def spread(layer, di):
        for dev in second.values():
            ag_copy(layer, at(di, 0), None, dev)

    def arrive(layer, di, dj):
        e = at(di, dj)
        last = dj or di
        if last == 2:
            ag_wait(layer, e, 0)
            ag_wait(layer, e, 1)
        elif last:
            ag_wait(layer, e, None)
        line = second if dj else first
        if last == 3:
            ag_copy(layer, e, 0, line[1])
        if last == 1:
            ag_copy(layer, e, 1, line[-1])
        ag_copy(layer, e, None, sib, pair=True)

    def own_out(layer):
        for dev in first.values():
            ag_copy(layer, me, None, dev)

    def pair_wait(layer, e):
        view = wb.at[layer, e]
        rdma(view, view, ag_send.at[0], ag_pair.at[layer, e], me).wait_recv()

    for copy in loads[:4]:
        copy.wait()
    own_out(0)
    spread(0, 0)
    arrive(0, 0, 0)
    xt[...] = x_ref[...].T
    dyt[...] = dy_ref[...].T
    acc[...] = xt[...].astype(F32)
    dxs[...] = dyt[...].astype(F32)
    dga_ref[...] = jnp.zeros_like(dga_ref)
    dgb_ref[...] = jnp.zeros_like(dgb_ref)
    for copy in loads[4:]:
        copy.wait()

    def actions(k, table):
        for step, todo in table.items():
            @pl.when(k == step)
            def _():
                for fn, *args in todo:
                    fn(*args)

    def pick(order, k):
        a, b = order(lax.div(k, side)), order(lax.rem(k, side))
        return at(a, b), member(lax.rem(r + a, side), lax.rem(p + b, side), 1 - core)

    def forward_one(e):
        _, gate, mask = route(e, ia_ref[...], ga_ref[...])
        o = expert_forward(wb[0, e], xt[...], mask)[5]
        acc[...] += gate * o.astype(F32)

    first_pass = {
        1: [(arrive, 0, 1, 0), (arrive, 0, 3, 0), (arrive, 0, 0, 1), (arrive, 0, 0, 3), (spread, 0, 1), (spread, 0, 3)],
        3: [(arrive, 0, 0, 2), (arrive, 0, 2, 0), (spread, 0, 2)],
        4: [(arrive, 0, 1, 1), (arrive, 0, 1, 3)],
        6: [(own_out, 1), (arrive, 1, 0, 0)],
        7: [(arrive, 0, 1, 2)],
        8: [(arrive, 0, 3, 1), (arrive, 0, 3, 3)],
        9: [(arrive, 1, 1, 0), (arrive, 1, 3, 0)],
        11: [(arrive, 0, 3, 2)],
        12: [(arrive, 0, 2, 1), (arrive, 0, 2, 3), (arrive, 1, 2, 0), (spread, 1, 2)],
        15: [(arrive, 0, 2, 2), (arrive, 1, 2, 1), (arrive, 1, 2, 3), (spread, 1, 1)],
    }
    second_pass = {
        0: [(arrive, 1, 2, 2)],
        2: [(spread, 1, 3)],
        3: [(arrive, 1, 1, 1), (arrive, 1, 1, 3)],
        4: [(arrive, 1, 1, 2)],
        6: [(spread, 1, 0)],
        7: [(arrive, 1, 3, 1), (arrive, 1, 3, 3)],
        8: [(arrive, 1, 3, 2)],
        11: [(arrive, 1, 0, 1), (arrive, 1, 0, 3)],
        12: [(arrive, 1, 0, 2)],
    }

    def forward_body(k, carry):
        actions(k, first_pass)
        own, other = pick(near_order, k)
        forward_one(own)
        pair_wait(0, other)
        forward_one(other)
        return carry

    lax.fori_loop(0, steps, forward_body, 0)
    xmt[...] = acc[...].astype(BF16)
    xm[...] = xmt[...].T
    acc[...] = xmt[...].astype(F32)

    def pair_send(layer, k):
        slot = lax.rem(k, ring)
        return rdma(dws.at[slot], rb.at[layer, k], d_send.at[slot], d_recv.at[layer, k], sib)

    def join(layer, k):
        pair_send(layer, k).wait_recv()
        dwo[layer, k] += rb[layer, k]

    lo, hi = pl.ds(0, gh), pl.ds(gh, gh)

    def far_copies(layer, g):
        return (rdma(dwo.at[layer, 4 * g, lo], ah.at[layer, g, 0], pa_send.at[layer, g, 0], ah_recv.at[layer, g, 0], second[1]),
                rdma(dwo.at[layer, 4 * g, hi], ah.at[layer, g, 1], pa_send.at[layer, g, 1], ah_recv.at[layer, g, 1], second[-1]))

    def near_copies(layer, g):
        return (rdma(dwo.at[layer, 4 * g + 1, hi], af.at[layer, g, 0, hi], pa_send.at[layer, g, 2], af_recv.at[layer, g, 0], second[1]),
                rdma(dwo.at[layer, 4 * g + 1, lo], af.at[layer, g, 0, lo], pa_send.at[layer, g, 3], af_recv.at[layer, g, 1], second[1]),
                rdma(dwo.at[layer, 4 * g + 2], af.at[layer, g, 1], pa_send.at[layer, g, 4], af_recv.at[layer, g, 2], second[-1]))

    def line_far(layer):
        return (rdma(dwo.at[layer, 3, lo], bh.at[layer, 0], pb_send.at[layer, 0], bh_recv.at[layer, 0], first[1]),
                rdma(dwo.at[layer, 3, hi], bh.at[layer, 1], pb_send.at[layer, 1], bh_recv.at[layer, 1], first[-1]))

    def line_near(layer):
        return (rdma(dwo.at[layer, 7], bf.at[layer, 0], pb_send.at[layer, 2], bf_recv.at[layer, 0], first[1]),
                rdma(dwo.at[layer, 11], bf.at[layer, 1], pb_send.at[layer, 3], bf_recv.at[layer, 1], first[-1]))

    def add_far(layer, g):
        for n, copy in enumerate(far_copies(layer, g)):
            copy.wait_recv()
            part = pl.ds(n * gh, gh)
            dwo[layer, 4 * g + 1 + n, part] += ah[layer, g, n]

    def add_near(layer, g):
        for copy in near_copies(layer, g):
            copy.wait_recv()
        dwo[layer, 4 * g + 3] += af[layer, g, 0] + af[layer, g, 1]

    def add_line(layer, n):
        line_far(layer)[n].wait_recv()
        part = pl.ds(n * gh, gh)
        dwo[layer, 7 + 4 * n, part] += bh[layer, n]

    def finish(layer, dw1, dw3, dw2):
        add_near(layer, 3)
        for copy in line_near(layer):
            copy.wait_recv()
        total = dwo[layer, 15] + bf[layer, 0] + bf[layer, 1]
        dw1[0] = total[:f].T
        dw3[0] = total[f : 2 * f].T
        dw2[0] = total[2 * f :]

    def middle(layer, k):
        g, part = lax.div(k, 4), lax.rem(k, 4)

        @pl.when(k >= 1)
        def _():
            join(layer, k - 1)

        @pl.when(part == 3)
        def _():
            add_far(layer, g)

        @pl.when((part == 2) & (k >= 6))
        def _():
            add_near(layer, g - 1)

        @pl.when(k == 10)
        def _():
            add_line(layer, 0)

        @pl.when(k == 14)
        def _():
            add_line(layer, 1)

    def end(layer, k):
        g, part = lax.div(k, 4), lax.rem(k, 4)

        @pl.when(part == 1)
        def _():
            for copy in far_copies(layer, g):
                copy.start()

        @pl.when(part == 2)
        def _():
            near_copies(layer, g)[0].start()

        @pl.when(part == 3)
        def _():
            for copy in near_copies(layer, g)[1:]:
                copy.start()

        @pl.when(k == 6)
        def _():
            for copy in line_far(layer):
                copy.start()

        @pl.when(k == 10)
        def _():
            line_near(layer)[0].start()

        @pl.when(k == 14)
        def _():
            line_near(layer)[1].start()

    def backward_one(layer, e, dst):
        idx, gates, dg = ((ia_ref, ga_ref, dga_ref), (ib_ref, gb_ref, dgb_ref))[layer]
        feat, rows = ((xt, x_ref), (xmt, xm))[layer]
        picked, gate, mask = route(e, idx[...], gates[...])
        w = wb[layer, e]
        parts = expert_forward(w, feat[...], mask)
        if layer:
            acc[...] += gate * parts[5].astype(F32)
        dgate, dw13_t, dw2, du = expert_backward(w, rows[...], dyt[...], gate, *parts)
        dg[...] += jnp.where(picked, dgate, 0.0)
        dst[: 2 * f] = dw13_t
        dst[2 * f :] = dw2
        dxs[...] += du.astype(F32)

    def backward_body(layer, k, carry):
        own, other = pick(far_order, k)
        if layer:
            actions(k, second_pass)
            pair_wait(1, other)

            @pl.when(k >= ring)
            def _():
                pair_send(layer, k).wait_send()
        else:
            pair_send(layer, k).wait_send()
        backward_one(layer, other, dws.at[lax.rem(k, ring)])
        middle(layer, k)
        if not layer:
            @pl.when(k == 0)
            def _():
                join(1, steps - 1)

            @pl.when(k == 3)
            def _():
                finish(1, dw1b, dw3b, dw2b)
        pair_send(layer, k).start()
        backward_one(layer, own, dwo.at[layer, k])
        end(layer, k)
        return carry

    lax.fori_loop(0, steps, functools.partial(backward_body, 1), 0)
    dyt[...] = dxs[...].astype(BF16)
    dxs[...] = dyt[...].astype(F32)
    xo_ref[...] = acc[...].astype(BF16).T
    lax.fori_loop(0, steps, functools.partial(backward_body, 0), 0)
    dxi_ref[...] = dxs[...].astype(BF16).T
    join(0, steps - 1)
    finish(0, dw1a, dw3a, dw2a)

    for n, half in enumerate(ag_slots):
        view = wb.at[0, 0] if half is None else wb.at[0, 0, pl.ds(0, wh)]
        rdma(view, view, ag_send.at[n], ag_recv.at[0, 0, 0], me).wait_send()
    for k in range(steps - ring, steps):
        pair_send(0, k).wait_send()
    for layer in range(2):
        for g in range(side):
            for copy in far_copies(layer, g) + near_copies(layer, g):
                copy.wait_send()
        for copy in line_far(layer) + line_near(layer):
            copy.wait_send()


def solution(mesh):
    tok_spec = P(("dp", "ep"))
    w_spec = P("ep")
    members = mesh.shape["ep"]
    side = math.isqrt(members // 2)
    chips = side * side

    def device_program(x_in, idx_a, idx_b, gate_a, gate_b, dy_out, w1_a, w3_a, w2_a, w1_b, w3_b, w2_b):
        (tok, d), top, f = x_in.shape, idx_a.shape[1], w1_a.shape[2]
        vmem, any_ = pl.BlockSpec(memory_space=pltpu.VMEM), pl.BlockSpec(memory_space=pl.ANY)
        shape = jax.ShapeDtypeStruct
        rows, dgs = shape((tok, d), BF16), shape((top, tok), F32)
        dws = (shape((1, d, f), F32), shape((1, d, f), F32), shape((1, f, d), F32))
        wrows, grows = 2 * d + 2 * f, 3 * f
        outs = pl.pallas_call(
            functools.partial(step_kernel, side),
            out_shape=(rows, rows) + dws + dws + (dgs, dgs),
            in_specs=[vmem] * 6 + [any_] * 6,
            out_specs=(vmem,) * 10,
            scratch_shapes=[
                pltpu.VMEM((2, members, wrows, f), BF16),
                pltpu.VMEM((2, chips, grows, d), F32),
                pltpu.VMEM((4, grows, d), F32),
                pltpu.VMEM((2, chips, grows, d), F32),
                pltpu.VMEM((2, side, 2, grows // 2, d), F32),
                pltpu.VMEM((2, side, 2, grows, d), F32),
                pltpu.VMEM((2, 2, grows // 2, d), F32),
                pltpu.VMEM((2, 2, grows, d), F32),
                pltpu.VMEM((d, tok), BF16),
                pltpu.VMEM((tok, d), BF16),
                pltpu.VMEM((d, tok), BF16),
                pltpu.VMEM((d, tok), BF16),
                pltpu.VMEM((d, tok), F32),
                pltpu.VMEM((d, tok), F32),
                pltpu.SemaphoreType.DMA((8,)),
                pltpu.SemaphoreType.DMA((72,)),
                pltpu.SemaphoreType.DMA((2, members, 2)),
                pltpu.SemaphoreType.DMA((2, members)),
                pltpu.SemaphoreType.DMA((4,)),
                pltpu.SemaphoreType.DMA((2, chips)),
                pltpu.SemaphoreType.DMA((2, side, 5)),
                pltpu.SemaphoreType.DMA((2, side, 2)),
                pltpu.SemaphoreType.DMA((2, side, 3)),
                pltpu.SemaphoreType.DMA((2, 4)),
                pltpu.SemaphoreType.DMA((2, 2)),
                pltpu.SemaphoreType.DMA((2, 2)),
            ],
            compiler_params=pltpu.CompilerParams(collective_id=0, has_side_effects=True, vmem_limit_bytes=62 * 2**20),
        )(x_in, dy_out, idx_a.T, idx_b.T, gate_a.T, gate_b.T, w1_a, w3_a, w2_a, w1_b, w3_b, w2_b)
        return outs[:8] + (outs[8].T, outs[9].T)

    return jax.shard_map(device_program, mesh=mesh, in_specs=(tok_spec,) * 6 + (w_spec,) * 6, out_specs=(tok_spec,) * 10, check_vma=False)
```

time: 347 us -> 172 us (0.50)
  waiting for transfers between devices: 225 us -> 0 us
  Pallas kernels: 90.4 us -> 162 us
  between operations: 13.8 us -> 0.68 us
    reduce_scatter x2 -> x0, waiting for transfers between devices: 153 us -> none  [the longest x1 96.3 us: device_program(): dw_a = lax.psum_scatter(dw_a, 'ep', scatter_dimension=0, tiled=True)]
    all_gather x2 -> x0, waiting for transfers between devices: 71.9 us -> none  [the longest x1 46.6 us: device_program(): w_a = lax.all_gather(pack(w1_a, w3_a, w2_a), 'ep')]
    pallas_call x3 -> x1, Pallas kernels: 90.4 us -> 162 us  [device_program(): pl.pallas_call(functools.partial(step_kernel, side), out_shape=(rows, row...]
    unnamed x22 -> x28, local copies, waits for them, and re-layouts: 7.79 us -> 9.51 us
  transfers between devices with their start and end apart: 4 -> 0, of which waited for: 4 -> 0; matrix products, arithmetic and copies ran while one was open for 2% -> 0% of each run, Pallas kernels for 15% -> 0%
where the time goes in v2:
time: 172 us
  Pallas kernels  162 us (94%)
  local copies, waits for them, and re-layouts  9.51 us (6%)
    pallas_call x1, Pallas kernels, device_program(): pl.pallas_call(functools.partial(step_kernel, side), out_shape=(rows, row...  162 us
    unnamed x28, local copies, waits for them, and re-layouts  9.51 us

profile of v2, /device:TPU:97, one launch (start us, length us, event | category | flops | bytes accessed | tf_op | source)
XLA Modules:
  0.0 171.8 jit_solution(5761360081427551106)
XLA Ops:
  0.6 161.6 %shard_map.195 = (bf16[512,256]{1,0:T(8,128)(2,1)}, bf16[512,256]{1,0:T(8,128)(2,1)}, f32[1,256,128]{2,1,0:T(8,128)}, f32[1,256,128]{2,1,0:T(8,128)}, f32[1,128,...) custom-call(bf16[512,256]{1,0:T(8,128)(2,1)} %x_ref.1, ...), custom_call_target="tpu_custom_call" | custom-call | tf_op jit(solution)/shard_map/pallas_call | solution.py:404
  162.3 0.0 copy-start
  162.3 1.7 copy.32
  164.0 0.0 copy-done
  164.0 0.0 copy-start.6
  164.0 0.7 copy.33
  164.7 0.3 copy-done.6
  165.0 0.0 copy-start.5
  165.0 0.7 copy.34
  165.7 0.3 copy-done.5
  166.0 0.0 copy-start.4
  166.0 0.7 copy.35
  166.6 0.3 copy-done.4
  166.9 0.0 copy-start.3
  166.9 0.7 copy.36
  167.6 0.3 copy-done.3
  167.9 0.0 copy-start.2
  167.9 0.7 copy.37
  168.5 0.3 copy-done.2
  168.8 0.0 copy-start.1
  168.8 0.7 copy.38
  169.5 0.3 copy-done.1
  169.8 0.0 copy-start.8
  169.8 0.7 copy.39
  170.4 0.1 copy-done.8
  170.5 0.0 copy-start.7
  170.5 0.6 copy.40
  171.1 0.1 copy-done.7
  171.2 0.6 copy.41
Async XLA Ops:
  162.3 1.7 %copy-start = (bf16[512,256]{1,0:T(8,128)(2,1)S(1)}, bf16[512,256]{1,0:T(8,128)(2,1)}, u32[]{:S(2)}) copy-start(bf16[512,256]{1,0:T(8,128)(2,1)} %get-tuple-element.41) | copy-start | bytes 786436
  164.0 1.0 copy-start.6
  165.0 1.0 copy-start.5
  166.0 1.0 copy-start.4
  166.9 1.0 copy-start.3
  167.9 1.0 copy-start.2
  168.8 1.0 copy-start.1
  169.8 0.7 copy-start.8
  170.5 0.7 copy-start.7

commit v3 on v2

--- a/solution.py
+++ b/solution.py
@@ -11,6 +11,40 @@
 F32 = jnp.float32
 BF16 = jnp.bfloat16
 MESH = pl.DeviceIdType.MESH
+
+PLAN = {
+    0: [("own_out", 1), ("spread", 0, 0), ("arrive", 0, 1, 0), ("arrive", 0, 3, 0), ("spread", 0, 1), ("arrive", 0, 0, 3)],
+    1: [("arrive", 1, 1, 0), ("arrive", 1, 3, 0)],
+    2: [("arrive", 0, 0, 1)],
+    3: [("spread", 0, 3)],
+    4: [("arrive", 0, 2, 0), ("spread", 0, 2)],
+    6: [("arrive", 0, 1, 3), ("arrive", 0, 0, 2)],
+    7: [("arrive", 0, 1, 1), ("arrive", 1, 2, 0)],
+    8: [("spread", 1, 2)],
+    9: [("arrive", 0, 3, 3)],
+    11: [("arrive", 0, 3, 1)],
+    12: [("arrive", 0, 2, 1)],
+    14: [("arrive", 0, 1, 2), ("arrive", 0, 2, 3)],
+    18: [("arrive", 1, 2, 3), ("arrive", 1, 2, 1)],
+    20: [("arrive", 0, 3, 2)],
+    21: [("spread", 1, 1)],
+    24: [("spread", 1, 0), ("spread", 1, 3)],
+    27: [("arrive", 0, 2, 2)],
+    28: [("arrive", 1, 2, 2)],
+    29: [("arrive", 1, 0, 0)],
+    33: [("arrive", 1, 1, 3), ("arrive", 1, 1, 1)],
+    34: [("arrive", 1, 0, 1)],
+    35: [("arrive", 1, 0, 3)],
+    37: [("arrive", 1, 3, 1)],
+    38: [("arrive", 1, 1, 2)],
+    39: [("arrive", 1, 3, 3)],
+    45: [("arrive", 1, 3, 2)],
+    48: [("arrive", 1, 0, 2)],
+}
+SUMS = (
+    {"far": 1, "near_up": 3, "near_down": 3, "join": 6, "line": 16, "last": 27},
+    {"far": 1, "near_up": 3, "near_down": 3, "join": 6, "line": 12, "last": 27},
+)
 
 
 def mm(a, b, ca, cb):
@@ -70,7 +104,7 @@
 
 
 def step_kernel(side, x_ref, dy_ref, ia_ref, ib_ref, ga_ref, gb_ref, w1a, w3a, w2a, w1b, w3b, w2b,
-                xo_ref, dxi_ref, dw1a, dw3a, dw2a, dw1b, dw3b, dw2b, dga_ref, dgb_ref,
+                xo_ref, dxi_ref, ta_ref, tb_ref, dga_ref, dgb_ref,
                 wb, dwo, dws, rb, ah, af, bh, bf, xt, xm, xmt, dyt, acc, dxs,
                 load_sem, ag_send, ag_recv, ag_pair, d_send, d_recv, pa_send, ah_recv, af_recv, pb_send, bh_recv, bf_recv):
     me = lax.axis_index("ep")
@@ -156,7 +190,6 @@
     for copy in loads[:4]:
         copy.wait()
     own_out(0)
-    spread(0, 0)
     arrive(0, 0, 0)
     xt[...] = x_ref[...].T
     dyt[...] = dy_ref[...].T
@@ -167,12 +200,16 @@
     for copy in loads[4:]:
         copy.wait()
 
-    def actions(k, table):
-        for step, todo in table.items():
-            @pl.when(k == step)
-            def _():
-                for fn, *args in todo:
-                    fn(*args)
+    moves = {"spread": spread, "arrive": arrive, "own_out": own_out}
+
+    def moves_at(k, base, half):
+        for step in range(steps):
+            todo = PLAN.get(base + 2 * step + half)
+            if todo:
+                @pl.when(k == step)
+                def _():
+                    for name, *args in todo:
+                        moves[name](*args)
 
     def pick(order, k):
         a, b = order(lax.div(k, side)), order(lax.rem(k, side))
@@ -183,34 +220,11 @@
         o = expert_forward(wb[0, e], xt[...], mask)[5]
         acc[...] += gate * o.astype(F32)
 
-    first_pass = {
-        1: [(arrive, 0, 1, 0), (arrive, 0, 3, 0), (arrive, 0, 0, 1), (arrive, 0, 0, 3), (spread, 0, 1), (spread, 0, 3)],
-        3: [(arrive, 0, 0, 2), (arrive, 0, 2, 0), (spread, 0, 2)],
-        4: [(arrive, 0, 1, 1), (arrive, 0, 1, 3)],
-        6: [(own_out, 1), (arrive, 1, 0, 0)],
-        7: [(arrive, 0, 1, 2)],
-        8: [(arrive, 0, 3, 1), (arrive, 0, 3, 3)],
-        9: [(arrive, 1, 1, 0), (arrive, 1, 3, 0)],
-        11: [(arrive, 0, 3, 2)],
-        12: [(arrive, 0, 2, 1), (arrive, 0, 2, 3), (arrive, 1, 2, 0), (spread, 1, 2)],
-        15: [(arrive, 0, 2, 2), (arrive, 1, 2, 1), (arrive, 1, 2, 3), (spread, 1, 1)],
-    }
-    second_pass = {
-        0: [(arrive, 1, 2, 2)],
-        2: [(spread, 1, 3)],
-        3: [(arrive, 1, 1, 1), (arrive, 1, 1, 3)],
-        4: [(arrive, 1, 1, 2)],
-        6: [(spread, 1, 0)],
-        7: [(arrive, 1, 3, 1), (arrive, 1, 3, 3)],
-        8: [(arrive, 1, 3, 2)],
-        11: [(arrive, 1, 0, 1), (arrive, 1, 0, 3)],
-        12: [(arrive, 1, 0, 2)],
-    }
-
     def forward_body(k, carry):
-        actions(k, first_pass)
         own, other = pick(near_order, k)
+        moves_at(k, 0, 0)
         forward_one(own)
+        moves_at(k, 0, 1)
         pair_wait(0, other)
         forward_one(other)
         return carry
@@ -235,9 +249,13 @@
                 rdma(dwo.at[layer, 4 * g, hi], ah.at[layer, g, 1], pa_send.at[layer, g, 1], ah_recv.at[layer, g, 1], second[-1]))
 
     def near_copies(layer, g):
-        return (rdma(dwo.at[layer, 4 * g + 1, hi], af.at[layer, g, 0, hi], pa_send.at[layer, g, 2], af_recv.at[layer, g, 0], second[1]),
-                rdma(dwo.at[layer, 4 * g + 1, lo], af.at[layer, g, 0, lo], pa_send.at[layer, g, 3], af_recv.at[layer, g, 1], second[1]),
-                rdma(dwo.at[layer, 4 * g + 2], af.at[layer, g, 1], pa_send.at[layer, g, 4], af_recv.at[layer, g, 2], second[-1]))
+        up, down = dwo.at[layer, 4 * g + 1], dwo.at[layer, 4 * g + 2]
+        up_in, down_in = af.at[layer, g, 0], af.at[layer, g, 1]
+        return tuple(
+            rdma(src.at[part], dst.at[part], pa_send.at[layer, g, 2 + n], af_recv.at[layer, g, n], dev)
+            for n, (src, dst, part, dev) in enumerate((
+                (up, up_in, hi, second[1]), (up, up_in, lo, second[1]),
+                (down, down_in, lo, second[-1]), (down, down_in, hi, second[-1]))))
 
     def line_far(layer):
         return (rdma(dwo.at[layer, 3, lo], bh.at[layer, 0], pb_send.at[layer, 0], bh_recv.at[layer, 0], first[1]),
@@ -263,67 +281,57 @@
         part = pl.ds(n * gh, gh)
         dwo[layer, 7 + 4 * n, part] += bh[layer, n]
 
-    def finish(layer, dw1, dw3, dw2):
+    def finish(layer, out):
         add_near(layer, 3)
         for copy in line_near(layer):
             copy.wait_recv()
-        total = dwo[layer, 15] + bf[layer, 0] + bf[layer, 1]
-        dw1[0] = total[:f].T
-        dw3[0] = total[f : 2 * f].T
-        dw2[0] = total[2 * f :]
-
-    def middle(layer, k):
-        g, part = lax.div(k, 4), lax.rem(k, 4)
-
-        @pl.when(k >= 1)
-        def _():
-            join(layer, k - 1)
-
-        @pl.when(part == 3)
-        def _():
-            add_far(layer, g)
-
-        @pl.when((part == 2) & (k >= 6))
-        def _():
-            add_near(layer, g - 1)
-
-        @pl.when(k == 10)
-        def _():
-            add_line(layer, 0)
-
-        @pl.when(k == 14)
-        def _():
-            add_line(layer, 1)
-
-    def end(layer, k):
-        g, part = lax.div(k, 4), lax.rem(k, 4)
-
-        @pl.when(part == 1)
-        def _():
-            for copy in far_copies(layer, g):
-                copy.start()
-
-        @pl.when(part == 2)
-        def _():
-            near_copies(layer, g)[0].start()
-
-        @pl.when(part == 3)
-        def _():
-            for copy in near_copies(layer, g)[1:]:
-                copy.start()
-
-        @pl.when(k == 6)
-        def _():
-            for copy in line_far(layer):
-                copy.start()
-
-        @pl.when(k == 10)
-        def _():
-            line_near(layer)[0].start()
-
-        @pl.when(k == 14)
-        def _():
-            line_near(layer)[1].start()
+        out[...] = dwo[layer, 15] + bf[layer, 0] + bf[layer, 1]
+
+    def when(cond, fn):
+        if isinstance(cond, bool):
+            if cond:
+                fn()
+        else:
+            pl.when(cond)(fn)
+
+    def each_group(kk, off, groups, fn):
+        if isinstance(kk, int):
+            if kk >= off and (kk - off) % 4 == 0 and (kk - off) // 4 < groups:
+                fn((kk - off) // 4)
+        else:
+            pl.when((kk >= off) & (lax.rem(kk - off + 32, 4) == 0) & (kk < off + 4 * groups))(lambda: fn(lax.div(kk - off, 4)))
+
+    def later(kk, first_step, last_step):
+        return isinstance(kk, int) or (first_step < steps if kk is sweep[0] else last_step >= steps)
+
+    def middle(layer, kk):
+        at_ = SUMS[layer]
+        if later(kk, at_["join"], at_["join"] + 12):
+            each_group(kk, at_["join"], 4, functools.partial(add_far, layer))
+        if later(kk, at_["line"], at_["line"] + 8):
+            each_group(kk, at_["line"], 3, functools.partial(add_near, layer))
+            when(kk == at_["line"] + 4, lambda: add_line(layer, 0))
+            when(kk == at_["line"] + 8, lambda: add_line(layer, 1))
+        if later(kk, at_["last"], at_["last"]):
+            when(kk == at_["last"], lambda: finish(layer, (ta_ref, tb_ref)[layer]))
+
+    def end(layer, kk):
+        at_ = SUMS[layer]
+
+        def start(copies, picks):
+            def go(*g):
+                made = copies(layer, *g)
+                for n in picks:
+                    made[n].start()
+            return go
+
+        for key, copies, picks in (("far", far_copies, (0, 1)), ("near_up", near_copies, (0,)), ("near_down", near_copies, (2,)), ("join", near_copies, (1, 3))):
+            if later(kk, at_[key], at_[key] + 12):
+                each_group(kk, at_[key], 4, start(copies, picks))
+        if later(kk, at_["line"], at_["line"] + 8):
+            when(kk == at_["line"], start(line_far, (0, 1)))
+            when(kk == at_["line"] + 4, start(line_near, (0,)))
+            when(kk == at_["line"] + 8, start(line_near, (1,)))
 
     def backward_one(layer, e, dst):
         idx, gates, dg = ((ia_ref, ga_ref, dga_ref), (ib_ref, gb_ref, dgb_ref))[layer]
@@ -339,10 +347,13 @@
         dst[2 * f :] = dw2
         dxs[...] += du.astype(F32)
 
+    sweep = [None]
+
     def backward_body(layer, k, carry):
+        sweep[0] = k
         own, other = pick(far_order, k)
         if layer:
-            actions(k, second_pass)
+            moves_at(k, 2 * steps, 0)
             pair_wait(1, other)
 
             @pl.when(k >= ring)
@@ -351,28 +362,30 @@
         else:
             pair_send(layer, k).wait_send()
         backward_one(layer, other, dws.at[lax.rem(k, ring)])
+        if not layer:
+            pl.when(k == 0)(lambda: join(1, steps - 1))
+            middle(1, k + steps)
+        pl.when(k >= 1)(lambda: join(layer, k - 1))
         middle(layer, k)
+        pair_send(layer, k).start()
+        if layer:
+            moves_at(k, 2 * steps, 1)
+        backward_one(layer, own, dwo.at[layer, k])
         if not layer:
-            @pl.when(k == 0)
-            def _():
-                join(1, steps - 1)
-
-            @pl.when(k == 3)
-            def _():
-                finish(1, dw1b, dw3b, dw2b)
-        pair_send(layer, k).start()
-        backward_one(layer, own, dwo.at[layer, k])
+            end(1, k + steps)
         end(layer, k)
         return carry
 
     lax.fori_loop(0, steps, functools.partial(backward_body, 1), 0)
     dyt[...] = dxs[...].astype(BF16)
     dxs[...] = dyt[...].astype(F32)
-    xo_ref[...] = acc[...].astype(BF16).T
+    xo_ref[...] = acc[...].astype(BF16)
     lax.fori_loop(0, steps, functools.partial(backward_body, 0), 0)
-    dxi_ref[...] = dxs[...].astype(BF16).T
+    dxi_ref[...] = dxs[...].astype(BF16)
     join(0, steps - 1)
-    finish(0, dw1a, dw3a, dw2a)
+    for kk in range(steps, SUMS[0]["last"] + 1):
+        middle(0, kk)
+        end(0, kk)
 
     for n, half in enumerate(ag_slots):
         view = wb.at[0, 0] if half is None else wb.at[0, 0, pl.ds(0, wh)]
@@ -387,6 +400,18 @@
             copy.wait_send()
 
 
+def finish_kernel(xo, dxi, ta, tb, dga, dgb, xo_ref, dxi_ref, dw1a, dw3a, dw2a, dw1b, dw3b, dw2b, dga_ref, dgb_ref):
+    xo_ref[...] = xo[...].T
+    dxi_ref[...] = dxi[...].T
+    for total, dw1, dw3, dw2 in ((ta, dw1a, dw3a, dw2a), (tb, dw1b, dw3b, dw2b)):
+        f = dw2.shape[1]
+        dw1[0] = total[:f].T
+        dw3[0] = total[f : 2 * f].T
+        dw2[0] = total[2 * f :]
+    dga_ref[...] = dga[...]
+    dgb_ref[...] = dgb[...]
+
+
 def solution(mesh):
     tok_spec = P(("dp", "ep"))
     w_spec = P("ep")
@@ -400,12 +425,13 @@
         shape = jax.ShapeDtypeStruct
         rows, dgs = shape((tok, d), BF16), shape((top, tok), F32)
         dws = (shape((1, d, f), F32), shape((1, d, f), F32), shape((1, f, d), F32))
+        cols = shape((d, tok), BF16)
         wrows, grows = 2 * d + 2 * f, 3 * f
         outs = pl.pallas_call(
             functools.partial(step_kernel, side),
-            out_shape=(rows, rows) + dws + dws + (dgs, dgs),
+            out_shape=(cols, cols, shape((grows, d), F32), shape((grows, d), F32), dgs, dgs),
             in_specs=[vmem] * 6 + [any_] * 6,
-            out_specs=(vmem,) * 10,
+            out_specs=(vmem,) * 6,
             scratch_shapes=[
                 pltpu.VMEM((2, members, wrows, f), BF16),
                 pltpu.VMEM((2, chips, grows, d), F32),
@@ -427,15 +453,21 @@
                 pltpu.SemaphoreType.DMA((2, members)),
                 pltpu.SemaphoreType.DMA((4,)),
                 pltpu.SemaphoreType.DMA((2, chips)),
-                pltpu.SemaphoreType.DMA((2, side, 5)),
+                pltpu.SemaphoreType.DMA((2, side, 6)),
                 pltpu.SemaphoreType.DMA((2, side, 2)),
-                pltpu.SemaphoreType.DMA((2, side, 3)),
+                pltpu.SemaphoreType.DMA((2, side, 4)),
                 pltpu.SemaphoreType.DMA((2, 4)),
                 pltpu.SemaphoreType.DMA((2, 2)),
                 pltpu.SemaphoreType.DMA((2, 2)),
             ],
             compiler_params=pltpu.CompilerParams(collective_id=0, has_side_effects=True, vmem_limit_bytes=62 * 2**20),
         )(x_in, dy_out, idx_a.T, idx_b.T, gate_a.T, gate_b.T, w1_a, w3_a, w2_a, w1_b, w3_b, w2_b)
-        return outs[:8] + (outs[8].T, outs[9].T)
+        outs = pl.pallas_call(
+            finish_kernel,
+            out_shape=(rows, rows) + dws + dws + (dgs, dgs),
+            in_specs=[vmem] * 6,
+            out_specs=(vmem,) * 10,
+        )(*outs)
+        return tuple(outs[:8]) + (outs[8].T, outs[9].T)
 
     return jax.shard_map(device_program, mesh=mesh, in_specs=(tok_spec,) * 6 + (w_spec,) * 6, out_specs=(tok_spec,) * 10, check_vma=False)

time: 172 us -> 127 us (0.74)
  Pallas kernels: 162 us -> 126 us
  local copies, waits for them, and re-layouts: 9.51 us -> 0 us
    pallas_call x1 -> x2, Pallas kernels: 162 us -> 126 us  [the longest x1 123 us: device_program(): pl.pallas_call(functools.partial(step_kernel, side), out_shape=(cols, col...]
    unnamed x28 -> x0, local copies, waits for them, and re-layouts: 9.51 us -> none
where the time goes in v3:
time: 127 us; the launch traced here: 126 us
  Pallas kernels  126 us (99%)
    pallas_call x1, Pallas kernels, device_program(): pl.pallas_call(functools.partial(step_kernel, side), out_shape=(cols, col...  123 us

profile of v3, /device:TPU:97, one launch (start us, length us, event | category | flops | bytes accessed | tf_op | source)
XLA Modules:
  0.0 126.3 jit_solution(18184441941306974665)
XLA Ops:
  0.6 123.2 %shard_map.195 = (bf16[256,512]{1,0:T(8,128)(2,1)}, bf16[256,512]{1,0:T(8,128)(2,1)}, f32[384,256]{1,0:T(8,128)}, f32[384,256]{1,0:T(8,128)}, f32[8,512]{1,0:T(8,128)}, /*index=5*/f32[8,512]{1,0:T(8,128)}) custom-call(bf16[512,256]{1,0:T(8,128)(2,1)} %x_ref.1, bf16[512,256]{1,0:T(8,128)(2,1)} %dy_ref.1, s32[8,512]{1,0:T(8,128)} %bitcast.6, ...), custom_call_target="tpu_custom_call" | custom-call | tf_op jit(solution)/shard_map/pallas_call | solution.py:430
  123.8 2.5 %shard_map.196 = (bf16[512,256]{1,0:T(8,128)(2,1)}, bf16[512,256]{1,0:T(8,128)(2,1)}, f32[1,256,128]{2,1,0:T(8,128)}, f32[1,256,128]{2,1,0:T(8,128)}, f32[1,128,...) custom-call(bf16[256,512]{1,0:T(8,128)(2,1)} %get-tuple-element.26.x, ...), custom_call_target="tpu_custom_call" | custom-call | tf_op jit(solution)/shard_map/pallas_call | solution.py:465

commit v4 on v3

--- a/solution.py
+++ b/solution.py
@@ -13,37 +13,28 @@
 MESH = pl.DeviceIdType.MESH
 
 PLAN = {
-    0: [("own_out", 1), ("spread", 0, 0), ("arrive", 0, 1, 0), ("arrive", 0, 3, 0), ("spread", 0, 1), ("arrive", 0, 0, 3)],
-    1: [("arrive", 1, 1, 0), ("arrive", 1, 3, 0)],
-    2: [("arrive", 0, 0, 1)],
-    3: [("spread", 0, 3)],
-    4: [("arrive", 0, 2, 0), ("spread", 0, 2)],
-    6: [("arrive", 0, 1, 3), ("arrive", 0, 0, 2)],
-    7: [("arrive", 0, 1, 1), ("arrive", 1, 2, 0)],
-    8: [("spread", 1, 2)],
-    9: [("arrive", 0, 3, 3)],
-    11: [("arrive", 0, 3, 1)],
-    12: [("arrive", 0, 2, 1)],
-    14: [("arrive", 0, 1, 2), ("arrive", 0, 2, 3)],
-    18: [("arrive", 1, 2, 3), ("arrive", 1, 2, 1)],
-    20: [("arrive", 0, 3, 2)],
-    21: [("spread", 1, 1)],
-    24: [("spread", 1, 0), ("spread", 1, 3)],
-    27: [("arrive", 0, 2, 2)],
-    28: [("arrive", 1, 2, 2)],
-    29: [("arrive", 1, 0, 0)],
-    33: [("arrive", 1, 1, 3), ("arrive", 1, 1, 1)],
-    34: [("arrive", 1, 0, 1)],
-    35: [("arrive", 1, 0, 3)],
-    37: [("arrive", 1, 3, 1)],
-    38: [("arrive", 1, 1, 2)],
-    39: [("arrive", 1, 3, 3)],
-    45: [("arrive", 1, 3, 2)],
-    48: [("arrive", 1, 0, 2)],
+    0: (100, 3, 30, 10, 1,),
+    1: (210, 230,),
+    2: (2, 110, 130,),
+    4: (11, 13,),
+    5: (20, 220, 120, 320,),
+    6: (33, 31,),
+    7: (12,),
+    8: (23,),
+    10: (21,),
+    11: (123, 121, 32, 310, 330,),
+    13: (22,),
+    15: (122,),
+    16: (111, 113,),
+    17: (300,),
+    18: (112, 133, 131,),
+    20: (103, 101,),
+    22: (132,),
+    26: (102,),
 }
 SUMS = (
-    {"far": 1, "near_up": 3, "near_down": 3, "join": 6, "line": 16, "last": 27},
-    {"far": 1, "near_up": 3, "near_down": 3, "join": 6, "line": 12, "last": 27},
+    {"far": 2, "near_up": 4, "near_down": 4, "join": 7, "line": 16, "last": 30},
+    {"far": 2, "near_up": 4, "near_down": 4, "join": 7, "line": 13, "last": 29},
 )
 
 
@@ -58,41 +49,59 @@
     return picked, gate, count > 0.5
 
 
-def expert_in(w, x_t, mask):
-    d = x_t.shape[0]
-    ab = mm(jnp.concatenate([w[:d], w[d : 2 * d]], axis=1), x_t, 0, 0)
-    ab = jnp.where(mask, ab, 0.0)
-    f = w.shape[1]
-    return ab[:f], ab[f:]
-
-
-def down(w, d):
+def up_rows(w, d):
+    return jnp.concatenate([w[:d], w[d : 2 * d]], axis=1)
+
+
+def down_rows(w, d):
     return jnp.concatenate([w[2 * d : 2 * d + d // 2], w[2 * d + d // 2 :]], axis=1)
 
 
-def expert_forward(w, x_t, mask):
-    d = x_t.shape[0]
-    a, b = expert_in(w, x_t, mask)
-    s = jax.nn.sigmoid(a)
-    silu = a * s
-    h = (silu * b).astype(BF16)
-    o = mm(down(w, d), h, 0, 0).astype(BF16)
-    return a, b, s, silu, h, o
-
-
-def expert_backward(w, x, dy_t, gate, a, b, s, silu, h, o):
-    d = x.shape[1]
-    dy = dy_t.astype(F32)
-    dgate = jnp.sum(dy * o.astype(F32), axis=0, keepdims=True)
-    q = (gate * dy).astype(BF16)
-    dh = mm(down(w, d), q, 1, 0)
-    dw2 = mm(h, q, 1, 1)
-    da = (dh * b * s * (1.0 + a * (1.0 - s))).astype(BF16)
-    db = (dh * silu).astype(BF16)
-    dab = jnp.concatenate([da, db], axis=0)
-    dw13_t = mm(dab, x, 1, 0)
-    du = mm(jnp.concatenate([w[:d], w[d : 2 * d]], axis=1), dab, 1, 0).astype(BF16)
-    return dgate, dw13_t, dw2, du
+def forward_pair(experts, idx_t, gate_t, x_t, acc, ab, hid):
+    d, f = x_t.shape[0], hid.shape[1]
+    gates = []
+    for n, w in enumerate(experts):
+        _, gate, mask = route(w[0], idx_t, gate_t)
+        gates.append(gate)
+        ab[n] = jnp.where(mask, mm(up_rows(w[1], d), x_t, 0, 0), 0.0)
+    for n in range(2):
+        for row in range(0, f, 16):
+            u = ab[n, row : row + 16]
+            hid[n, row : row + 16] = (u * jax.nn.sigmoid(u) * ab[n, f + row : f + row + 16]).astype(BF16)
+    parts = [gates[n] * mm(down_rows(w[1], d), hid[n], 0, 0).astype(BF16).astype(F32) for n, w in enumerate(experts)]
+    acc[...] += parts[0] + parts[1]
+
+
+def backward_pair(experts, idx_t, gate_t, x_t, x, dy_t, acc, dxs, dg, ab, hid, dhs, dab, q):
+    d, f = x_t.shape[0], hid.shape[1]
+    gates, picks = [], []
+    for n, (e, w, _) in enumerate(experts):
+        picked, gate, mask = route(e, idx_t, gate_t)
+        gates.append(gate)
+        picks.append(picked)
+        q[n] = (gate * dy_t[...].astype(F32)).astype(BF16)
+        ab[n] = jnp.where(mask, mm(up_rows(w, d), x_t[...], 0, 0), 0.0)
+        dhs[n] = mm(down_rows(w, d), q[n], 1, 0)
+    for n in range(2):
+        for row in range(0, f, 16):
+            u, v = ab[n, row : row + 16], ab[n, f + row : f + row + 16]
+            dh = dhs[n, row : row + 16]
+            s = jax.nn.sigmoid(u)
+            silu = u * s
+            hid[n, row : row + 16] = (silu * v).astype(BF16)
+            dab[n, row : row + 16] = (dh * v * s * (1.0 + u * (1.0 - s))).astype(BF16)
+            dab[n, f + row : f + row + 16] = (dh * silu).astype(BF16)
+    for n, (e, w, dst) in enumerate(experts):
+        dst[: 2 * f] = mm(dab[n], x[...], 1, 0)
+        dst[2 * f :] = mm(hid[n], q[n], 1, 1)
+    outs = [mm(down_rows(w, d), hid[n], 0, 0).astype(BF16).astype(F32) for n, (e, w, _) in enumerate(experts)]
+    if acc is not None:
+        acc[...] += gates[0] * outs[0] + gates[1] * outs[1]
+    dy = dy_t[...].astype(F32)
+    for n in range(2):
+        dg[...] += jnp.where(picks[n], jnp.sum(dy * outs[n], axis=0, keepdims=True), 0.0)
+    dus = [mm(up_rows(w, d), dab[n], 1, 0).astype(BF16).astype(F32) for n, (e, w, _) in enumerate(experts)]
+    dxs[...] += dus[0] + dus[1]
 
 
 def near_order(g):
@@ -105,7 +114,7 @@
 
 def step_kernel(side, x_ref, dy_ref, ia_ref, ib_ref, ga_ref, gb_ref, w1a, w3a, w2a, w1b, w3b, w2b,
                 xo_ref, dxi_ref, ta_ref, tb_ref, dga_ref, dgb_ref,
-                wb, dwo, dws, rb, ah, af, bh, bf, xt, xm, xmt, dyt, acc, dxs,
+                wb, dwo, dws, rb, ah, af, bh, bf, xt, xm, xmt, dyt, acc, dxs, ab, hid, dhs, dab, q,
                 load_sem, ag_send, ag_recv, ag_pair, d_send, d_recv, pa_send, ah_recv, af_recv, pb_send, bh_recv, bf_recv):
     me = lax.axis_index("ep")
     core, chip = lax.rem(me, 2), lax.div(me, 2)
@@ -191,6 +200,7 @@
         copy.wait()
     own_out(0)
     arrive(0, 0, 0)
+    spread(0, 0)
     xt[...] = x_ref[...].T
     dyt[...] = dy_ref[...].T
     acc[...] = xt[...].astype(F32)
@@ -200,33 +210,32 @@
     for copy in loads[4:]:
         copy.wait()
 
-    moves = {"spread": spread, "arrive": arrive, "own_out": own_out}
-
-    def moves_at(k, base, half):
+    def moves_at(k, base):
         for step in range(steps):
-            todo = PLAN.get(base + 2 * step + half)
+            todo = PLAN.get(base + step)
             if todo:
                 @pl.when(k == step)
                 def _():
-                    for name, *args in todo:
-                        moves[name](*args)
+                    for code in todo:
+                        kind, block = divmod(code, 100)
+                        kind, layer = divmod(kind, 2)
+                        di, dj = divmod(block, 10)
+                        if kind == 1:
+                            spread(layer, di)
+                        else:
+                            if not block:
+                                own_out(layer)
+                            arrive(layer, di, dj)
 
     def pick(order, k):
         a, b = order(lax.div(k, side)), order(lax.rem(k, side))
         return at(a, b), member(lax.rem(r + a, side), lax.rem(p + b, side), 1 - core)
 
-    def forward_one(e):
-        _, gate, mask = route(e, ia_ref[...], ga_ref[...])
-        o = expert_forward(wb[0, e], xt[...], mask)[5]
-        acc[...] += gate * o.astype(F32)
-
     def forward_body(k, carry):
+        moves_at(k, 0)
         own, other = pick(near_order, k)
-        moves_at(k, 0, 0)
-        forward_one(own)
-        moves_at(k, 0, 1)
         pair_wait(0, other)
-        forward_one(other)
+        forward_pair([(e, wb[0, e]) for e in (own, other)], ia_ref[...], ga_ref[...], xt[...], acc, ab, hid)
         return carry
 
     lax.fori_loop(0, steps, forward_body, 0)
@@ -333,27 +342,13 @@
             when(kk == at_["line"] + 4, start(line_near, (0,)))
             when(kk == at_["line"] + 8, start(line_near, (1,)))
 
-    def backward_one(layer, e, dst):
-        idx, gates, dg = ((ia_ref, ga_ref, dga_ref), (ib_ref, gb_ref, dgb_ref))[layer]
-        feat, rows = ((xt, x_ref), (xmt, xm))[layer]
-        picked, gate, mask = route(e, idx[...], gates[...])
-        w = wb[layer, e]
-        parts = expert_forward(w, feat[...], mask)
-        if layer:
-            acc[...] += gate * parts[5].astype(F32)
-        dgate, dw13_t, dw2, du = expert_backward(w, rows[...], dyt[...], gate, *parts)
-        dg[...] += jnp.where(picked, dgate, 0.0)
-        dst[: 2 * f] = dw13_t
-        dst[2 * f :] = dw2
-        dxs[...] += du.astype(F32)
-
     sweep = [None]
 
     def backward_body(layer, k, carry):
         sweep[0] = k
         own, other = pick(far_order, k)
         if layer:
-            moves_at(k, 2 * steps, 0)
+            moves_at(k, steps)
             pair_wait(1, other)
 
             @pl.when(k >= ring)
@@ -361,19 +356,17 @@
                 pair_send(layer, k).wait_send()
         else:
             pair_send(layer, k).wait_send()
-        backward_one(layer, other, dws.at[lax.rem(k, ring)])
-        if not layer:
-            pl.when(k == 0)(lambda: join(1, steps - 1))
+            pl.when(k < 2)(lambda: join(1, k + steps - 2))
             middle(1, k + steps)
-        pl.when(k >= 1)(lambda: join(layer, k - 1))
+        pl.when(k >= 2)(lambda: join(layer, k - 2))
         middle(layer, k)
-        pair_send(layer, k).start()
-        if layer:
-            moves_at(k, 2 * steps, 1)
-        backward_one(layer, own, dwo.at[layer, k])
+        experts = [(other, wb[layer, other], dws.at[lax.rem(k, ring)]), (own, wb[layer, own], dwo.at[layer, k])]
+        idx, gates, dg, feat, rows = ((ia_ref, ga_ref, dga_ref, xt, x_ref), (ib_ref, gb_ref, dgb_ref, xmt, xm))[layer]
+        backward_pair(experts, idx[...], gates[...], feat, rows, dyt, acc if layer else None, dxs, dg, ab, hid, dhs, dab, q)
         if not layer:
             end(1, k + steps)
         end(layer, k)
+        pair_send(layer, k).start()
         return carry
 
     lax.fori_loop(0, steps, functools.partial(backward_body, 1), 0)
@@ -382,8 +375,9 @@
     xo_ref[...] = acc[...].astype(BF16)
     lax.fori_loop(0, steps, functools.partial(backward_body, 0), 0)
     dxi_ref[...] = dxs[...].astype(BF16)
-    join(0, steps - 1)
     for kk in range(steps, SUMS[0]["last"] + 1):
+        if kk < steps + 2:
+            join(0, kk - 2)
         middle(0, kk)
         end(0, kk)
 
@@ -447,6 +441,11 @@
                 pltpu.VMEM((d, tok), BF16),
                 pltpu.VMEM((d, tok), F32),
                 pltpu.VMEM((d, tok), F32),
+                pltpu.VMEM((2, 2 * f, tok), F32),
+                pltpu.VMEM((2, f, tok), BF16),
+                pltpu.VMEM((2, f, tok), F32),
+                pltpu.VMEM((2, 2 * f, tok), BF16),
+                pltpu.VMEM((2, d, tok), BF16),
                 pltpu.SemaphoreType.DMA((8,)),
                 pltpu.SemaphoreType.DMA((72,)),
                 pltpu.SemaphoreType.DMA((2, members, 2)),

time: 127 us -> 118 us (0.929)
  Pallas kernels: 126 us -> 117 us
    pallas_call x1, Pallas kernels: 123 us -> 115 us  [device_program(): pl.pallas_call(functools.partial(step_kernel, side), out_shape=(cols, col...]
where the time goes in v4:
time: 118 us
  Pallas kernels  117 us (99%)
    pallas_call x1, Pallas kernels, device_program(): pl.pallas_call(functools.partial(step_kernel, side), out_shape=(cols, col...  115 us
    pallas_call x1, Pallas kernels, device_program(): pl.pallas_call(finish_kernel, out_shape=(rows, rows) + dws + dws + (dgs,...  2.46 us

profile of v4, /device:TPU:97, one launch (start us, length us, event | category | flops | bytes accessed | tf_op | source)
XLA Modules:
  0.0 118.0 jit_solution(12260930637640473126)
XLA Ops:
  0.6 114.9 %shard_map.195 = (bf16[256,512]{1,0:T(8,128)(2,1)}, bf16[256,512]{1,0:T(8,128)(2,1)}, f32[384,256]{1,0:T(8,128)}, f32[384,256]{1,0:T(8,128)}, f32[8,512]{1,0:T(8,128)}, /*index=5*/f32[8,512]{1,0:T(8,128)}) custom-call(bf16[512,256]{1,0:T(8,128)(2,1)} %x_ref.1, bf16[512,256]{1,0:T(8,128)(2,1)} %dy_ref.1, s32[8,512]{1,0:T(8,128)} %bitcast.6, ...), custom_call_target="tpu_custom_call" | custom-call | tf_op jit(solution)/shard_map/pallas_call | solution.py:424
  115.6 2.5 %shard_map.196 = (bf16[512,256]{1,0:T(8,128)(2,1)}, bf16[512,256]{1,0:T(8,128)(2,1)}, f32[1,256,128]{2,1,0:T(8,128)}, f32[1,256,128]{2,1,0:T(8,128)}, f32[1,128,...) custom-call(bf16[256,512]{1,0:T(8,128)(2,1)} %get-tuple-element.26.x, ...), custom_call_target="tpu_custom_call" | custom-call | tf_op jit(solution)/shard_map/pallas_call | solution.py:464
